TPU v7x, 256 devices: a whole 4x4x8 slice. The times are simulated.
256 devices in a mesh: px: 2 (over core), py: 8 (over z), ta: 16 (over y, x).
Axes of the slice: x: 4, y: 4, z: 8, core: 2. Of those that a mesh axis runs over, the one named last changes fastest.
Arguments:
- snapshots: bfloat16 [384, 5, 131072], P('ta', None, ('px', 'py')), may hold values from -6 to 6
- quad_weights: float32 [131072], P(('px', 'py')), may hold values from 1 to 10
- spectral_indices: int32 [32], replicated, may hold values from 0 to 127
Outputs:
- spectra: float32 [32, 2, 2, 5, 131072], P('ta', None, None, None, ('px', 'py'))
- gram: float32 [32, 2, 2, 2], P('ta')
All inputs are finite; a program needn't handle non-finite values.
Results may differ from a plain program's by a relative error of at most 0.0042.
Values may be sent and summed in bfloat16 or wider, within the bound.
A program may use at most 128 MiB of HBM per device.

v0:
```python
import math

import jax
import jax.numpy as jnp
from jax import lax
from jax.sharding import PartitionSpec as P

VARS = 5
BLK = 256
HOP = 128
SEGMENT_NUMBER = 2
RECORD_LENGTH = 384
RETAINED_MODES = 32


def copy_for_each(shard, axis):
    devices = lax.axis_size(axis)
    return lax.all_to_all(
        jnp.broadcast_to(shard[None], (devices, *shard.shape)), axis, 0, 0, tiled=True
    )


def of_everyone(shard, axis):
    return copy_for_each(shard, axis).sum(axis=0)


def make_rotation_multipliers(spectral_indices, temporal_locations):
    segment_beginnings = jnp.arange(SEGMENT_NUMBER, dtype=jnp.int32) * HOP
    segment_shifts = temporal_locations[None, :] - segment_beginnings[:, None]
    inside = (segment_shifts >= 0) & (segment_shifts < BLK)
    window = 0.5 - 0.5 * jnp.cos(2.0 * math.pi * segment_shifts.astype(jnp.float32) / BLK)
    window = jnp.where(inside, window, jnp.float32(0.0)) / jnp.sqrt(jnp.float32(3.0 * BLK / 8.0))
    phases = jnp.mod(spectral_indices[:, None, None] * segment_shifts[None, :, :], BLK)
    angles = 2.0 * math.pi * phases.astype(jnp.float32) / BLK
    real_part = jnp.cos(angles) * window[None]
    imag_part = -jnp.sin(angles) * window[None]
    gathered_segments = jnp.stack([real_part, imag_part], axis=2)
    return gathered_segments.reshape(
        RETAINED_MODES * SEGMENT_NUMBER * 2, temporal_locations.shape[0]
    ).astype(jnp.bfloat16)


def gram_terms(spectra):
    flat = spectra.reshape(spectra.shape[0], 2 * SEGMENT_NUMBER, -1)
    inner = jnp.einsum("fam,fbm->fab", flat, flat, precision=lax.Precision.HIGHEST)
    inner = inner.reshape(spectra.shape[0], SEGMENT_NUMBER, 2, SEGMENT_NUMBER, 2)
    real_part = inner[:, :, 0, :, 0] + inner[:, :, 1, :, 1]
    imag_part = inner[:, :, 0, :, 1] - inner[:, :, 1, :, 0]
    return jnp.stack([real_part, imag_part], axis=-1)


def on_device(snapshots, quad_weights, spectral_indices):
    point_count = snapshots.shape[2]
    groups = lax.axis_size("ta")
    temporal_locations = jnp.arange(RECORD_LENGTH, dtype=jnp.int32)
    rotation_multipliers = make_rotation_multipliers(spectral_indices, temporal_locations)
    local_spectra = jnp.einsum(
        "rt,tvp->rvp",
        rotation_multipliers,
        lax.all_to_all(snapshots, "ta", split_axis=2, concat_axis=0, tiled=True),
        preferred_element_type=jnp.float32,
    )
    raw = lax.all_to_all(
        local_spectra.astype(jnp.bfloat16), "ta", split_axis=0, concat_axis=2, tiled=True
    ).astype(local_spectra.dtype)
    raw = raw.reshape(RETAINED_MODES // groups, SEGMENT_NUMBER, 2, VARS, point_count)
    spectra = raw * jnp.sqrt(quad_weights)
    summed = of_everyone(gram_terms(spectra), ("px", "py"))
    total_points = point_count * lax.axis_size("px") * lax.axis_size("py")
    gram = summed / jnp.float32(total_points * VARS)
    return (spectra, gram)


def solution(mesh):
    return jax.shard_map(
        on_device,
        mesh=mesh,
        in_specs=(P("ta", None, ("px", "py")), P(("px", "py")), P()),
        out_specs=(P("ta", None, None, None, ("px", "py")), P("ta", None, None, None)),
        check_vma=False,
    )
```

profile of v0, /device:TPU:1, one launch (start us, length us, event | category | flops | bytes accessed | tf_op | source)
XLA Modules:
  0.0 153.8 jit_solution(5036630691097740982)
XLA Ops:
  0.6 14.4 %copy.48 = bf16[24,5,8192]{0,1,2:T(8,128)(2,1)} copy(bf16[24,5,8192]{2,0,1:T(8,128)(2,1)} %param.3) | data formatting | bytes 3932160 | tf_op args[0]
  15.0 19.3 %reshape.183 = bf16[16,2,30720]{2,1,0:T(2,128)(2,1)} reshape(bf16[8192,5,24]{2,1,0:T(8,128)(2,1)} %bitcast.24) | data formatting | bytes 3932160
  34.4 0.0 copy-start.1
  34.4 7.7 %all-to-all-start = ((bf16[16,2,30720]{2,1,0:T(2,128)(2,1)}), bf16[16,2,30720]{2,1,0:T(2,128)(2,1)S(1)}, u32[]{:S(2)}, u32[]{:S(2)}) async-start(bf16[16,2,30720]{2,1,0:T(2,128)(2,1)} %reshape.183), calls=%async_computation | async-start | bytes 3932160 | tf_op jit(solution)/shard_map/all_to_all | solution.py:60
  42.1 0.1 fusion.8
  42.2 0.1 iota_subtract_fusion
  42.3 0.0 copy-done.1
  42.3 0.5 multiply_convert_fusion.1
  42.8 0.1 copy.47
  43.0 28.0 %all-to-all-done = bf16[16,2,30720]{2,1,0:T(2,128)(2,1)S(1)} async-done(((bf16[16,2,30720]{2,1,0:T(2,128)(2,1)}), bf16[16,2,30720]{2,1,0:T(2,128)(2,1)S(1)}, u32[]{:S(2)}, u32[]{:S(2)}) %all-to-all-start) | async-done | bytes 1966112 | tf_op jit(solution)/shard_map/all_to_all | solution.py:60
  70.9 15.5 %reshape.184 = bf16[8192,5,24]{2,1,0:T(8,128)(2,1)} reshape(bf16[16,2,30720]{2,1,0:T(2,128)(2,1)S(1)} %all-to-all-done) | data formatting | bytes 3932160
  86.4 14.6 %copy.49 = bf16[24,5,16,512]{3,0,2,1:T(8,128)(2,1)S(1)} copy(bf16[24,5,16,512]{0,1,3,2:T(8,128)(2,1)} %bitcast.23) | data formatting | bytes 3932160 | tf_op jit(solution)/shard_map/all_to_all | solution.py:60
  101.0 0.5 convolution_convert_fusion
  101.5 1.3 copy.50
  102.8 0.0 copy-start
  102.8 4.3 %all-to-all-start.1 = ((bf16[128,5,512]{2,1,0:T(8,128)(2,1)}), bf16[128,5,512]{2,1,0:T(8,128)(2,1)S(1)}, u32[]{:S(2)}, u32[]{:S(2)}) async-start(bf16[128,5,512]{2,1,0:T(8,128)(2,1)} %copy.50), calls=%async_computation.1 | async-start | bytes 2097152 | tf_op jit(solution)/shard_map/all_to_all | solution.py:63
  107.2 0.0 copy-done
  107.2 0.7 mul.107
  108.0 14.7 %all-to-all-done.1 = bf16[128,5,512]{2,1,0:T(8,128)(2,1)S(1)} async-done(((bf16[128,5,512]{2,1,0:T(8,128)(2,1)}), bf16[128,5,512]{2,1,0:T(8,128)(2,1)S(1)}, u32[]{:S(2)}, u32[]{:S(2)}) %all-to-all-start.1) | async-done | bytes 655392 | tf_op jit(solution)/shard_map/all_to_all | solution.py:63
  122.7 1.5 copy.59
  124.2 0.3 convert_bitcast_fusion
  124.5 2.2 %reshape.176 = f32[2,4,40960]{2,1,0:T(4,128)S(1)} reshape(f32[8,5,16,512]{3,2,1,0:T(8,128)} %bitcast.28) | data formatting | bytes 2621440 | tf_op jit(solution)/shard_map/convert_element_type | solution.py:65
  126.7 6.8 %fusion = f32[2,4,4]{2,1,0:T(4,128)S(1)} fusion(f32[2,4,40960]{2,1,0:T(4,128)S(1)} %reshape.176, f32[40960]{0:T(1024)} %mul.107), kind=kOutput, calls=%fused_computation.2 | convolution fusion | flops 16056320 | bytes 1474688 | tf_op jit(solution)/shard_map/fam,fbm->fab/dot_general | solution.py:45
  133.5 0.1 reshape.174
  133.6 0.2 fusion.7
  133.8 0.1 copy.53
  133.9 0.6 broadcast_in_dim.7
  134.6 11.5 %all-to-all-start.2 = ((f32[16,2,2,2,2]{4,3,2,1,0:T(2,128)}), f32[16,2,2,2,2]{4,3,2,1,0:T(2,128)S(1)}, u32[]{:S(2)}, u32[]{:S(2)}) async-start(f32[16,2,2,2,2]{4,3,2,1,0:T(2,128)} %broadcast_in_dim.7), calls=%async_computation.2 | async-start | bytes 131072 | tf_op jit(solution)/shard_map/all_to_all | solution.py:18
  146.0 0.8 copy.52
  146.8 1.1 reshape.175
  147.9 0.5 broadcast_multiply_fusion
  148.5 1.1 copy.55
  149.6 3.5 %all-to-all-done.2 = f32[16,2,2,2,2]{4,3,2,1,0:T(2,128)S(1)} async-done(((f32[16,2,2,2,2]{4,3,2,1,0:T(2,128)}), f32[16,2,2,2,2]{4,3,2,1,0:T(2,128)S(1)}, u32[]{:S(2)}, u32[]{:S(2)}) %all-to-all-start.2) | async-done | bytes 1056 | tf_op jit(solution)/shard_map/all_to_all | solution.py:18
  153.2 0.6 broadcast_multiply_fusion.1
  (7 shorter events, 0.1 us)
Async XLA Ops:
  34.4 7.9 %copy-start.1 = (s32[32]{0:T(128)S(1)}, s32[32]{0:T(128)}, u32[]{:S(2)}) copy-start(s32[32]{0:T(128)} %param.5) | copy-start | bytes 388
  34.4 36.5 %all-to-all-start = ((bf16[16,2,30720]{2,1,0:T(2,128)(2,1)}), bf16[16,2,30720]{2,1,0:T(2,128)(2,1)S(1)}, u32[]{:S(2)}, u32[]{:S(2)}) async-start(bf16[16,2,30720]{2,1,0:T(2,128)(2,1)} %reshape.183), calls=%async_computation | async-start | bytes 3932160 | tf_op jit(solution)/shard_map/all_to_all | solution.py:60
  102.8 4.3 %copy-start = (f32[8192]{0:T(1024)S(1)}, f32[8192]{0:T(1024)}, u32[]{:S(2)}) copy-start(f32[8192]{0:T(1024)} %param.4) | copy-start | bytes 98308
  102.8 19.9 %all-to-all-start.1 = ((bf16[128,5,512]{2,1,0:T(8,128)(2,1)}), bf16[128,5,512]{2,1,0:T(8,128)(2,1)S(1)}, u32[]{:S(2)}, u32[]{:S(2)}) async-start(bf16[128,5,512]{2,1,0:T(8,128)(2,1)} %copy.50), calls=%async_computation.1 | async-start | bytes 2097152 | tf_op jit(solution)/shard_map/all_to_all | solution.py:63
  134.6 18.6 %all-to-all-start.2 = ((f32[16,2,2,2,2]{4,3,2,1,0:T(2,128)}), f32[16,2,2,2,2]{4,3,2,1,0:T(2,128)S(1)}, u32[]{:S(2)}, u32[]{:S(2)}) async-start(f32[16,2,2,2,2]{4,3,2,1,0:T(2,128)} %broadcast_in_dim.7), calls=%async_computation.2 | async-start | bytes 131072 | tf_op jit(solution)/shard_map/all_to_all | solution.py:18
where the time goes:
time: 155 us; the launch traced here: 154 us
  local copies, waits for them, and re-layouts  73.6 us (47%)
  waiting for transfers between devices  46.2 us (30%)
  starting transfers between devices  23.5 us (15%)
  matrix products  7.34 us (5%)
  other arithmetic  2.34 us (2%)
    unnamed x8, local copies, waits for them, and re-layouts  50.4 us
    all_to_all x1, waiting for transfers between devices, on_device(): lax.all_to_all(snapshots, 'ta', split_axis=2, concat_axis=0, tiled=True)  28 us
    all_to_all x1, waiting for transfers between devices, on_device(): lax.all_to_all(local_spectra.astype(jnp.bfloat16), 'ta', split_axis=0, co...  14.7 us
    all_to_all x1, local copies, waits for them, and re-layouts, on_device(): lax.all_to_all(snapshots, 'ta', split_axis=2, concat_axis=0, tiled=True)  14.6 us
    all_to_all x1, starting transfers between devices, copy_for_each(): lax.all_to_all(jnp.broadcast_to(shard[None], (devices, *shard.shape)), ax...  11.5 us
    all_to_all x1, starting transfers between devices, on_device(): lax.all_to_all(snapshots, 'ta', split_axis=2, concat_axis=0, tiled=True)  7.7 us
    dot_general x1, matrix products, gram_terms(): jnp.einsum('fam,fbm->fab', flat, flat, precision=lax.Precision.HIGHEST)  6.84 us
    convert_element_type x4, local copies, waits for them, and re-layouts, on_device(): raw = lax.all_to_all(local_spectra.astype(jnp.bfloat16), 'ta', split_axis...  5.6 us
  transfers between devices with their start and end apart: 3, of which 3 were waited for; matrix products, arithmetic and copies ran while one was open for 3% of the time, Pallas kernels for 0%

commit v1 on v0

v1 whole, which is shorter than its diff:
```python
import functools
import math

import jax
import jax.numpy as jnp
from jax import lax
from jax.experimental import pallas as pl
from jax.experimental.pallas import tpu as pltpu
from jax.sharding import PartitionSpec as P

VARS = 5
BLK = 256
HOP = 128
SEGMENT_NUMBER = 2
RECORD_LENGTH = 384
RETAINED_MODES = 32
ROWS = RETAINED_MODES * SEGMENT_NUMBER * 2
MESH = pl.DeviceIdType.MESH
LANES = 128
STEPS = (
    (0, 1), (0, 3), (1, 0), (3, 0), (0, 2), (2, 0), (1, 1), (3, 3),
    (1, 3), (3, 1), (2, 1), (2, 3), (1, 2), (3, 2), (2, 2),
)


def cosine(phase):
    k = jnp.bitwise_and(phase, BLK - 1)
    k = jnp.where(k > BLK // 2, BLK - k, k)
    far = k > BLK // 4
    k = jnp.where(far, BLK // 2 - k, k)
    a = k.astype(jnp.float32) * jnp.float32(2.0 * math.pi / BLK)
    s = a * a
    total = jnp.float32(1.0 / math.factorial(12))
    for n in (10, 8, 6, 4, 2, 0):
        total = total * s * -1.0 if n == 10 else total * s
        total = total + jnp.float32((-1.0) ** (n // 2) / math.factorial(n))
    return jnp.where(far, -total, total)


def exchange_kernel(
    groups, width, cores, depth,
    snap, weights, indices, out, gram_out,
    mine, arrived, twiddles, terms, staged, w_ref, idx_ref, squares, crosses, gram_mine, gram_seen, gram_sum,
    load_sem, own_sem, small_sem, send_sem, recv_sem, send_two, recv_two, gram_send, gram_recv, last_send, last_recv,
):
    me = lax.axis_index("ta")
    px, py = lax.axis_index("px"), lax.axis_index("py")
    side = math.isqrt(groups)
    y, x = me // side, me % side
    peers = [lax.rem(y + dy, side) * side + lax.rem(x + dx, side) for dy, dx in STEPS]
    place = px * depth + py
    others = [(dp, dz) for dz in range(depth) for dp in range(cores) if (dp, dz) != (0, 0)]
    planes = [(lax.rem(px + dp, cores), lax.rem(py + dz, depth)) for dp, dz in others]

    index_copy = pltpu.make_async_copy(indices, idx_ref, small_sem.at[0])
    index_copy.start()
    weight_copy = pltpu.make_async_copy(weights, w_ref, small_sem.at[1])
    weight_copy.start()
    loads = [pltpu.make_async_copy(snap.at[v], mine.at[v], load_sem.at[v]) for v in range(VARS)]
    for load in loads:
        load.start()
    own = pl.ds(pl.multiple_of(me * width, LANES), width)
    for v in range(VARS):
        pltpu.make_async_copy(snap.at[v, :, own], arrived.at[v, me], own_sem.at[v]).start()

    barrier = pltpu.get_barrier_semaphore()
    for peer in peers:
        pl.semaphore_signal(barrier, inc=1, device_id={"ta": peer}, device_id_type=MESH)
    for p, z in planes:
        pl.semaphore_signal(barrier, inc=1, device_id={"px": p, "py": z}, device_id_type=MESH)

    index_copy.wait()
    shape = (8, RECORD_LENGTH)
    row = lax.broadcasted_iota(jnp.int32, shape, 0)
    lag = lax.broadcasted_iota(jnp.int32, shape, 1) - HOP * jnp.bitwise_and(row // 2, 1)
    turn = (BLK // 4) * jnp.bitwise_and(row, 1)
    inside = (lag >= 0) & (lag < BLK)
    window = jnp.float32(0.5) - jnp.float32(0.5) * cosine(lag)
    window = jnp.where(inside, window, jnp.float32(0.0)) / jnp.sqrt(jnp.float32(3.0 * BLK / 8.0))

    def fill(g, carry):
        index = jnp.where(row < 4, idx_ref[2 * g], idx_ref[2 * g + 1])
        rows = pl.ds(pl.multiple_of(g * 8, 8), 8)
        twiddles[rows, :] = cosine(index * lag + turn) * window
        squares[rows, :] = jnp.zeros((8, LANES), jnp.float32)
        crosses[rows, :] = jnp.zeros((8, LANES), jnp.float32)
        return carry

    lax.fori_loop(0, ROWS // 8, fill, 0)
    weight_copy.wait()
    for load in loads:
        load.wait()
    pl.semaphore_wait(barrier, len(peers) + len(planes))

    def to_owner(v, peer):
        cut = pl.ds(pl.multiple_of(peer * width, LANES), width)
        return pltpu.make_async_remote_copy(
            src_ref=mine.at[v, :, cut], dst_ref=arrived.at[v, me], send_sem=send_sem.at[v], recv_sem=recv_sem.at[v],
            device_id={"ta": peer}, device_id_type=MESH,
        )

    def send_all(v, carry):
        for peer in peers:
            to_owner(v, peer).start()
        return carry

    lax.fori_loop(0, VARS, send_all, 0)
    line = lax.broadcasted_iota(jnp.int32, (8, LANES), 0)
    quarter = jnp.bitwise_and(line, 3)

    def work(v, carry):
        pltpu.make_async_copy(arrived.at[v, pl.ds(0, groups - 1)], arrived.at[v, pl.ds(0, groups - 1)], recv_sem.at[v]).wait()
        pltpu.make_async_copy(snap.at[v, :, own], arrived.at[v, me], own_sem.at[v]).wait()
        series = arrived[v].reshape(RECORD_LENGTH, width)
        raw = jnp.dot(twiddles[...].astype(jnp.bfloat16), series, preferred_element_type=jnp.float32)
        terms[...] = raw
        staged[v] = raw.astype(jnp.bfloat16).reshape(groups, 8, width)

        def gather(g, inner):
            rows = pl.ds(pl.multiple_of(g * 8, 8), 8)
            square = squares[rows, :]
            cross = crosses[rows, :]
            for j in range(width // LANES):
                a = terms[rows, j * LANES : (j + 1) * LANES]
                w = w_ref[pl.ds(me * (width // LANES) + j, 1), :]
                first = jnp.where(quarter < 2, a, pltpu.roll(a, 2, 0))
                second = jnp.where(quarter < 2, pltpu.roll(a, 6, 0), jnp.where(quarter == 2, pltpu.roll(a, 7, 0), pltpu.roll(a, 1, 0)))
                square = square + a * a * w
                cross = cross + first * second * w
            squares[rows, :] = square
            crosses[rows, :] = cross
            return inner

        lax.fori_loop(0, ROWS // 8, gather, 0)
        for peer in peers:
            pltpu.make_async_remote_copy(
                src_ref=staged.at[v, peer], dst_ref=out.at[v, me], send_sem=send_two.at[v], recv_sem=recv_two.at[v],
                device_id={"ta": peer}, device_id_type=MESH,
            ).start()
        out[v, me] = staged[v, me]
        return carry

    lax.fori_loop(0, VARS, work, 0)

    diagonal = lax.broadcasted_iota(jnp.int32, (ROWS, LANES), 0) == lax.broadcasted_iota(jnp.int32, (ROWS, LANES), 1)

    def in_lanes(ref):
        sums = jnp.sum(ref[...], axis=1, keepdims=True)
        return jnp.sum(jnp.where(diagonal, sums, jnp.float32(0.0)), axis=0, keepdims=True)

    both = jnp.where(line == 0, in_lanes(squares), in_lanes(crosses))
    gram_mine[...] = both
    gram_seen[place] = both
    for i, (p, z) in enumerate(planes):
        pltpu.make_async_remote_copy(
            src_ref=gram_mine, dst_ref=gram_seen.at[place], send_sem=gram_send, recv_sem=gram_recv,
            device_id={"px": p, "py": z}, device_id_type=MESH,
        ).start()
    n_planes = len(planes)
    pltpu.make_async_copy(gram_seen.at[pl.ds(0, n_planes)], gram_seen.at[pl.ds(0, n_planes)], gram_recv).wait()
    whole = jnp.sum(gram_seen[...], axis=0)
    gram_sum[...] = whole
    gram_out[me] = whole
    for peer in peers:
        pltpu.make_async_remote_copy(
            src_ref=gram_sum, dst_ref=gram_out.at[me], send_sem=last_send, recv_sem=last_recv,
            device_id={"ta": peer}, device_id_type=MESH,
        ).start()

    n = len(peers)
    for v in range(VARS):
        pltpu.make_async_copy(out.at[v, pl.ds(0, n)], out.at[v, pl.ds(0, n)], recv_two.at[v]).wait()
    pltpu.make_async_copy(gram_out.at[pl.ds(0, n)], gram_out.at[pl.ds(0, n)], last_recv).wait()
    for v in range(VARS):
        pltpu.make_async_copy(arrived.at[v, pl.ds(0, n)], arrived.at[v, pl.ds(0, n)], send_sem.at[v]).wait()
        pltpu.make_async_copy(out.at[v, pl.ds(0, n)], out.at[v, pl.ds(0, n)], send_two.at[v]).wait()
    pltpu.make_async_copy(gram_seen.at[pl.ds(0, n_planes)], gram_seen.at[pl.ds(0, n_planes)], gram_send).wait()
    pltpu.make_async_copy(gram_out.at[pl.ds(0, n)], gram_out.at[pl.ds(0, n)], last_send).wait()


def finish_kernel(groups, width, total, held, w_ref, gram_in, out, gram):
    def scale(k, carry):
        lanes = pl.ds(pl.multiple_of(k * width, LANES), width)
        for j in range(width // LANES):
            root = jnp.sqrt(w_ref[pl.ds(k * (width // LANES) + j, 1), :])
            part = held[0, k, :, j * LANES : (j + 1) * LANES].astype(jnp.float32) * root
            at = pl.ds(pl.multiple_of(k * width + j * LANES, LANES), LANES)
            for i in range(4):
                out[i, 0, :, at] = part[2 * i : 2 * i + 2, :]
        return carry

    lax.fori_loop(0, groups, scale, 0)

    @pl.when(pl.program_id(0) == 0)
    def _():
        me = lax.axis_index("ta")
        sums = jnp.sum(gram_in[...], axis=0) / jnp.float32(total)
        sums = pltpu.roll(sums, lax.rem(LANES - 8 * me, LANES), 1)
        r = lax.broadcasted_iota(jnp.int32, (2, 2), 0)
        c = lax.broadcasted_iota(jnp.int32, (2, 2), 1)

        def entry(kind, lane):
            return jnp.broadcast_to(sums[kind : kind + 1, lane : lane + 1], (2, 2))

        zero = jnp.zeros((2, 2), jnp.float32)
        for f in range(2):
            real = entry(1, 4 * f) + entry(1, 4 * f + 1)
            imag = entry(1, 4 * f + 2) - entry(1, 4 * f + 3)
            for b in range(2):
                power = entry(0, 4 * f + 2 * b) + entry(0, 4 * f + 2 * b + 1)
                crossed = jnp.where(c == 0, real, imag if b == 0 else -imag)
                gram[f, b] = jnp.where(r == b, jnp.where(c == 0, power, zero), crossed)


def solution(mesh):
    groups, cores, depth = mesh.shape["ta"], mesh.shape["px"], mesh.shape["py"]

    def on_device(snapshots, quad_weights, spectral_indices):
        steps, _, points = snapshots.shape
        width = points // groups
        series = jnp.transpose(snapshots, (1, 0, 2))
        weights = quad_weights.reshape(points // LANES, LANES)
        anywhere = pl.BlockSpec(memory_space=pl.ANY)
        vmem = pl.BlockSpec(memory_space=pltpu.VMEM)
        held, gram_parts = pl.pallas_call(
            functools.partial(exchange_kernel, groups, width, cores, depth),
            name="exchange",
            out_shape=(
                jax.ShapeDtypeStruct((VARS, groups, 8, width), jnp.bfloat16),
                jax.ShapeDtypeStruct((groups, 8, LANES), jnp.float32),
            ),
            in_specs=[anywhere, anywhere, anywhere],
            out_specs=(vmem, vmem),
            scratch_shapes=[
                pltpu.VMEM((VARS, steps, points), jnp.bfloat16),
                pltpu.VMEM((VARS, groups, steps, width), jnp.bfloat16),
                pltpu.VMEM((ROWS, RECORD_LENGTH), jnp.float32),
                pltpu.VMEM((ROWS, width), jnp.float32),
                pltpu.VMEM((VARS, groups, 8, width), jnp.bfloat16),
                pltpu.VMEM((points // LANES, LANES), jnp.float32),
                pltpu.SMEM((RETAINED_MODES,), jnp.int32),
                pltpu.VMEM((ROWS, LANES), jnp.float32),
                pltpu.VMEM((ROWS, LANES), jnp.float32),
                pltpu.VMEM((8, LANES), jnp.float32),
                pltpu.VMEM((cores * depth, 8, LANES), jnp.float32),
                pltpu.VMEM((8, LANES), jnp.float32),
                pltpu.SemaphoreType.DMA((VARS,)),
                pltpu.SemaphoreType.DMA((VARS,)),
                pltpu.SemaphoreType.DMA((2,)),
                pltpu.SemaphoreType.DMA((VARS,)),
                pltpu.SemaphoreType.DMA((VARS,)),
                pltpu.SemaphoreType.DMA((VARS,)),
                pltpu.SemaphoreType.DMA((VARS,)),
                pltpu.SemaphoreType.DMA,
                pltpu.SemaphoreType.DMA,
                pltpu.SemaphoreType.DMA,
                pltpu.SemaphoreType.DMA,
            ],
            compiler_params=pltpu.CompilerParams(collective_id=0, has_side_effects=True, vmem_limit_bytes=32 * 2**20),
        )(series, weights, spectral_indices)
        total = points * cores * depth * VARS
        spectra, gram = pl.pallas_call(
            functools.partial(finish_kernel, groups, width, total),
            name="finish",
            grid=(VARS,),
            out_shape=(
                jax.ShapeDtypeStruct((4, VARS, 2, points), jnp.float32),
                jax.ShapeDtypeStruct((2, 2, 2, 2), jnp.float32),
            ),
            in_specs=[pl.BlockSpec((1, groups, 8, width), lambda v: (v, 0, 0, 0)), vmem, vmem],
            out_specs=(
                pl.BlockSpec((4, 1, 2, points), lambda v: (0, v, 0, 0)),
                vmem,
            ),
        )(held, weights, gram_parts)
        spectra = spectra.reshape(2, SEGMENT_NUMBER, VARS, 2, points).transpose(0, 1, 3, 2, 4)
        return (spectra, gram)

    return jax.shard_map(
        on_device,
        mesh=mesh,
        in_specs=(P("ta", None, ("px", "py")), P(("px", "py")), P()),
        out_specs=(P("ta", None, None, None, ("px", "py")), P("ta", None, None, None)),
        check_vma=False,
    )
```

time: 155 us -> 58.2 us (0.38)
  local copies, waits for them, and re-layouts: 73.6 us -> 4.4 us
  Pallas kernels: 0 us -> 52.9 us
  waiting for transfers between devices: 46.2 us -> 0 us
  starting transfers between devices: 23.5 us -> 0 us
  matrix products: 7.34 us -> 0 us
  other arithmetic: 2.34 us -> 0 us
    pallas_call x0 -> x2, Pallas kernels: none -> 52.9 us  [the longest x1 48.1 us: on_device(): pl.pallas_call(functools.partial(exchange_kernel, groups, width, cores, d...]
    all_to_all x3 -> x0, waiting for transfers between devices: 46.2 us -> none  [the longest x1 28 us: on_device(): lax.all_to_all(snapshots, 'ta', split_axis=2, concat_axis=0, tiled=True)]
    unnamed x8 -> x10, local copies, waits for them, and re-layouts: 50.4 us -> 4.4 us
    all_to_all x3 -> x0, starting transfers between devices: 23.5 us -> none  [the longest x1 11.5 us: copy_for_each(): lax.all_to_all(jnp.broadcast_to(shard[None], (devices, *shard.shape)), ax...]
    all_to_all x1 -> x0, local copies, waits for them, and re-layouts: 14.6 us -> none  [on_device(): lax.all_to_all(snapshots, 'ta', split_axis=2, concat_axis=0, tiled=True)]
    dot_general x2 -> x0, matrix products: 7.34 us -> none  [the longest x1 6.84 us: gram_terms(): jnp.einsum('fam,fbm->fab', flat, flat, precision=lax.Precision.HIGHEST)]
    convert_element_type x6 -> x0, local copies, waits for them, and re-layouts: 6.99 us -> none  [the longest x4 5.6 us: on_device(): raw = lax.all_to_all(local_spectra.astype(jnp.bfloat16), 'ta', split_axis...]
  transfers between devices with their start and end apart: 3 -> 0, of which waited for: 3 -> 0; matrix products, arithmetic and copies ran while one was open for 3% -> 0% of each run, Pallas kernels for 0% -> 0%
where the time goes in v1:
time: 58.2 us; the launch traced here: 58 us
  Pallas kernels  52.9 us (91%)
  local copies, waits for them, and re-layouts  4.4 us (8%)
  between operations  0.66 us (1%)
    pallas_call x1, Pallas kernels, on_device(): pl.pallas_call(functools.partial(exchange_kernel, groups, width, cores, d...  48.1 us
    pallas_call x1, Pallas kernels, on_device(): pl.pallas_call(functools.partial(finish_kernel, groups, width, total), na...  4.77 us
    unnamed x10, local copies, waits for them, and re-layouts  4.4 us

profile of v1, /device:TPU:1, one launch (start us, length us, event | category | flops | bytes accessed | tf_op | source)
XLA Modules:
  0.0 58.0 jit_solution(8158817627138936678)
XLA Ops:
  0.6 0.0 copy-start
  0.6 1.5 %copy-done = bf16[24,5,8192]{2,0,1:T(8,128)(2,1)S(1)} copy-done((bf16[24,5,8192]{2,0,1:T(8,128)(2,1)S(1)}, bf16[24,5,8192]{2,0,1:T(8,128)(2,1)}, u32[]{:S(2)}) %copy-start) | copy-done | bytes 1966104
  2.2 0.0 copy-start.2
  2.2 0.8 %copy-done.2 = f32[8192]{0:T(1024)S(1)} copy-done((f32[8192]{0:T(1024)S(1)}, f32[8192]{0:T(1024)}, u32[]{:S(2)}) %copy-start.2) | copy-done | bytes 32792
  2.9 0.0 copy-start.4
  2.9 0.7 %copy-done.4 = s32[32]{0:T(128)S(1)} copy-done((s32[32]{0:T(128)S(1)}, s32[32]{0:T(128)}, u32[]{:S(2)}) %copy-start.4) | copy-done | bytes 152
  3.6 48.1 %exchange.1 = (bf16[5,16,8,512]{3,2,1,0:T(8,128)(2,1)S(1)}, f32[16,8,128]{2,1,0:T(8,128)S(1)}) custom-call(bf16[5,24,8192]{2,1,0:T(8,128)(2,1)S(1)} %bitcast.5, f32[64,128]{1,0:T(8,128)S(1)} %bitcast.7, s32[32]{0:T(128)S(1)} %copy-done.4), custom_call_target="tpu_custom_call" | custom-call | tf_op jit(solution)/shard_map/exchange/pallas_call | solution.py:225
  51.7 0.0 copy-start.1
  51.7 0.8 %copy-done.1 = bf16[5,16,8,512]{3,2,1,0:T(8,128)(2,1)} copy-done((bf16[5,16,8,512]{3,2,1,0:T(8,128)(2,1)}, bf16[5,16,8,512]{3,2,1,0:T(8,128)(2,1)S(1)}, u32[]{:S(2)}) %copy-start.1) | copy-done | bytes 655384
  52.6 0.0 copy-start.3
  52.6 0.6 %copy-done.3 = f32[16,8,128]{2,1,0:T(8,128)} copy-done((f32[16,8,128]{2,1,0:T(8,128)}, f32[16,8,128]{2,1,0:T(8,128)S(1)}, u32[]{:S(2)}) %copy-start.3) | copy-done | bytes 65560
  53.2 4.8 %finish.1 = (f32[4,5,2,8192]{3,2,1,0:T(2,128)}, f32[2,2,2,2]{3,2,1,0:T(2,128)}) custom-call(bf16[5,16,8,512]{3,2,1,0:T(8,128)(2,1)} %copy-done.1, f32[64,128]{1,0:T(8,128)} %bitcast.6, f32[16,8,128]{2,1,0:T(8,128)} %copy-done.3), custom_call_target="tpu_custom_call" | custom-call | tf_op jit(solution)/shard_map/finish/pallas_call | solution.py:262
Async XLA Ops:
  0.6 1.5 %copy-start = (bf16[24,5,8192]{2,0,1:T(8,128)(2,1)S(1)}, bf16[24,5,8192]{2,0,1:T(8,128)(2,1)}, u32[]{:S(2)}) copy-start(bf16[24,5,8192]{2,0,1:T(8,128)(2,1)} %param.3) | copy-start | bytes 5898244
  2.2 0.8 %copy-start.2 = (f32[8192]{0:T(1024)S(1)}, f32[8192]{0:T(1024)}, u32[]{:S(2)}) copy-start(f32[8192]{0:T(1024)} %param.4) | copy-start | bytes 98308
  2.9 0.7 %copy-start.4 = (s32[32]{0:T(128)S(1)}, s32[32]{0:T(128)}, u32[]{:S(2)}) copy-start(s32[32]{0:T(128)} %indices.1) | copy-start | bytes 388
  51.7 0.8 %copy-start.1 = (bf16[5,16,8,512]{3,2,1,0:T(8,128)(2,1)}, bf16[5,16,8,512]{3,2,1,0:T(8,128)(2,1)S(1)}, u32[]{:S(2)}) copy-start(bf16[5,16,8,512]{3,2,1,0:T(8,128)(2,1)S(1)} %get-tuple-element.6.held) | copy-start | bytes 1966084
  52.6 0.6 %copy-start.3 = (f32[16,8,128]{2,1,0:T(8,128)}, f32[16,8,128]{2,1,0:T(8,128)S(1)}, u32[]{:S(2)}) copy-start(f32[16,8,128]{2,1,0:T(8,128)S(1)} %get-tuple-element.7.gram_in) | copy-start | bytes 196612

commit v2 on v1

--- a/solution.py
+++ b/solution.py
@@ -39,8 +39,8 @@
 
 def exchange_kernel(
     groups, width, cores, depth,
-    snap, weights, indices, out, gram_out,
-    mine, arrived, twiddles, terms, staged, w_ref, idx_ref, squares, crosses, gram_mine, gram_seen, gram_sum,
+    snap, weights, indices, spectra, gram_out,
+    mine, arrived, twiddles, terms, staged, out, w_ref, roots, idx_ref, squares, crosses, gram_mine, gram_seen, gram_sum,
     load_sem, own_sem, small_sem, send_sem, recv_sem, send_two, recv_two, gram_send, gram_recv, last_send, last_recv,
 ):
     me = lax.axis_index("ta")
@@ -168,8 +168,25 @@
         ).start()
 
     n = len(peers)
-    for v in range(VARS):
+    tiles = width // LANES
+    roots[...] = jnp.sqrt(w_ref[...])
+
+    def scale(v, carry):
         pltpu.make_async_copy(out.at[v, pl.ds(0, n)], out.at[v, pl.ds(0, n)], recv_two.at[v]).wait()
+
+        def one(k, inner):
+            for j in range(tiles):
+                root = roots[pl.ds(k * tiles + j, 1), :]
+                part = out[v, k, :, j * LANES : (j + 1) * LANES].astype(jnp.float32) * root
+                at = pl.ds(pl.multiple_of(k * width + j * LANES, LANES), LANES)
+                for i in range(4):
+                    spectra[i, v, :, at] = part[2 * i : 2 * i + 2, :]
+            return inner
+
+        lax.fori_loop(0, groups, one, 0)
+        return carry
+
+    lax.fori_loop(0, VARS, scale, 0)
     pltpu.make_async_copy(gram_out.at[pl.ds(0, n)], gram_out.at[pl.ds(0, n)], last_recv).wait()
     for v in range(VARS):
         pltpu.make_async_copy(arrived.at[v, pl.ds(0, n)], arrived.at[v, pl.ds(0, n)], send_sem.at[v]).wait()
@@ -178,38 +195,29 @@
     pltpu.make_async_copy(gram_out.at[pl.ds(0, n)], gram_out.at[pl.ds(0, n)], last_send).wait()
 
 
-def finish_kernel(groups, width, total, held, w_ref, gram_in, out, gram):
-    def scale(k, carry):
-        lanes = pl.ds(pl.multiple_of(k * width, LANES), width)
-        for j in range(width // LANES):
-            root = jnp.sqrt(w_ref[pl.ds(k * (width // LANES) + j, 1), :])
-            part = held[0, k, :, j * LANES : (j + 1) * LANES].astype(jnp.float32) * root
-            at = pl.ds(pl.multiple_of(k * width + j * LANES, LANES), LANES)
-            for i in range(4):
-                out[i, 0, :, at] = part[2 * i : 2 * i + 2, :]
-        return carry
-
-    lax.fori_loop(0, groups, scale, 0)
-
-    @pl.when(pl.program_id(0) == 0)
-    def _():
-        me = lax.axis_index("ta")
-        sums = jnp.sum(gram_in[...], axis=0) / jnp.float32(total)
-        sums = pltpu.roll(sums, lax.rem(LANES - 8 * me, LANES), 1)
-        r = lax.broadcasted_iota(jnp.int32, (2, 2), 0)
-        c = lax.broadcasted_iota(jnp.int32, (2, 2), 1)
-
-        def entry(kind, lane):
-            return jnp.broadcast_to(sums[kind : kind + 1, lane : lane + 1], (2, 2))
-
-        zero = jnp.zeros((2, 2), jnp.float32)
-        for f in range(2):
-            real = entry(1, 4 * f) + entry(1, 4 * f + 1)
-            imag = entry(1, 4 * f + 2) - entry(1, 4 * f + 3)
-            for b in range(2):
-                power = entry(0, 4 * f + 2 * b) + entry(0, 4 * f + 2 * b + 1)
-                crossed = jnp.where(c == 0, real, imag if b == 0 else -imag)
-                gram[f, b] = jnp.where(r == b, jnp.where(c == 0, power, zero), crossed)
+def finish_kernel(total, spectra, gram_in, out, gram, sem):
+    copies = [pltpu.make_async_copy(spectra.at[i], out.at[i], sem.at[i]) for i in range(4)]
+    for copy in copies:
+        copy.start()
+    me = lax.axis_index("ta")
+    sums = jnp.sum(gram_in[...], axis=0) / jnp.float32(total)
+    sums = pltpu.roll(sums, lax.rem(LANES - 8 * me, LANES), 1)
+    r = lax.broadcasted_iota(jnp.int32, (2, 2), 0)
+    c = lax.broadcasted_iota(jnp.int32, (2, 2), 1)
+
+    def entry(kind, lane):
+        return jnp.broadcast_to(sums[kind : kind + 1, lane : lane + 1], (2, 2))
+
+    zero = jnp.zeros((2, 2), jnp.float32)
+    for f in range(2):
+        real = entry(1, 4 * f) + entry(1, 4 * f + 1)
+        imag = entry(1, 4 * f + 2) - entry(1, 4 * f + 3)
+        for b in range(2):
+            power = entry(0, 4 * f + 2 * b) + entry(0, 4 * f + 2 * b + 1)
+            crossed = jnp.where(c == 0, real, imag if b == 0 else -imag)
+            gram[f, b] = jnp.where(r == b, jnp.where(c == 0, power, zero), crossed)
+    for copy in copies:
+        copy.wait()
 
 
 def solution(mesh):
@@ -220,16 +228,16 @@
         width = points // groups
         series = jnp.transpose(snapshots, (1, 0, 2))
         weights = quad_weights.reshape(points // LANES, LANES)
-        anywhere = pl.BlockSpec(memory_space=pl.ANY)
+        hbm = pl.BlockSpec(memory_space=pltpu.HBM)
         vmem = pl.BlockSpec(memory_space=pltpu.VMEM)
-        held, gram_parts = pl.pallas_call(
+        spectra, gram_parts = pl.pallas_call(
             functools.partial(exchange_kernel, groups, width, cores, depth),
             name="exchange",
             out_shape=(
-                jax.ShapeDtypeStruct((VARS, groups, 8, width), jnp.bfloat16),
+                jax.ShapeDtypeStruct((4, VARS, 2, points), jnp.float32),
                 jax.ShapeDtypeStruct((groups, 8, LANES), jnp.float32),
             ),
-            in_specs=[anywhere, anywhere, anywhere],
+            in_specs=[hbm, hbm, hbm],
             out_specs=(vmem, vmem),
             scratch_shapes=[
                 pltpu.VMEM((VARS, steps, points), jnp.bfloat16),
@@ -237,6 +245,8 @@
                 pltpu.VMEM((ROWS, RECORD_LENGTH), jnp.float32),
                 pltpu.VMEM((ROWS, width), jnp.float32),
                 pltpu.VMEM((VARS, groups, 8, width), jnp.bfloat16),
+                pltpu.VMEM((VARS, groups, 8, width), jnp.bfloat16),
+                pltpu.VMEM((points // LANES, LANES), jnp.float32),
                 pltpu.VMEM((points // LANES, LANES), jnp.float32),
                 pltpu.SMEM((RETAINED_MODES,), jnp.int32),
                 pltpu.VMEM((ROWS, LANES), jnp.float32),
@@ -257,22 +267,20 @@
                 pltpu.SemaphoreType.DMA,
             ],
             compiler_params=pltpu.CompilerParams(collective_id=0, has_side_effects=True, vmem_limit_bytes=32 * 2**20),
-        )(series, weights, spectral_indices)
+        )(*(pltpu.with_memory_space_constraint(a, pltpu.HBM) for a in (series, weights, spectral_indices)))
         total = points * cores * depth * VARS
         spectra, gram = pl.pallas_call(
-            functools.partial(finish_kernel, groups, width, total),
+            functools.partial(finish_kernel, total),
             name="finish",
-            grid=(VARS,),
             out_shape=(
                 jax.ShapeDtypeStruct((4, VARS, 2, points), jnp.float32),
                 jax.ShapeDtypeStruct((2, 2, 2, 2), jnp.float32),
             ),
-            in_specs=[pl.BlockSpec((1, groups, 8, width), lambda v: (v, 0, 0, 0)), vmem, vmem],
-            out_specs=(
-                pl.BlockSpec((4, 1, 2, points), lambda v: (0, v, 0, 0)),
-                vmem,
-            ),
-        )(held, weights, gram_parts)
+            in_specs=[vmem, vmem],
+            out_specs=(hbm, vmem),
+            scratch_shapes=[pltpu.SemaphoreType.DMA((4,))],
+            compiler_params=pltpu.CompilerParams(vmem_limit_bytes=8 * 2**20),
+        )(spectra, gram_parts)
         spectra = spectra.reshape(2, SEGMENT_NUMBER, VARS, 2, points).transpose(0, 1, 3, 2, 4)
         return (spectra, gram)
 

time: 58.2 us -> 49.8 us (0.86)
  local copies, waits for them, and re-layouts: 4.4 us -> 0 us
  Pallas kernels: 52.9 us -> 49 us
    unnamed x10 -> x0, local copies, waits for them, and re-layouts: 4.4 us -> none
    pallas_call x1, Pallas kernels: 4.77 us -> 1.68 us  [on_device(): pl.pallas_call(functools.partial(finish_kernel, total), name='finish', ou...]
    pallas_call x1, Pallas kernels: 48.1 us -> 47.4 us  [on_device(): pl.pallas_call(functools.partial(exchange_kernel, groups, width, cores, d...]
where the time goes in v2:
time: 49.8 us; the launch traced here: 49.7 us
  Pallas kernels  49 us (98%)
  between operations  0.64 us (1%)
    pallas_call x1, Pallas kernels, on_device(): pl.pallas_call(functools.partial(exchange_kernel, groups, width, cores, d...  47.4 us
    pallas_call x1, Pallas kernels, on_device(): pl.pallas_call(functools.partial(finish_kernel, total), name='finish', ou...  1.68 us

profile of v2, /device:TPU:1, one launch (start us, length us, event | category | flops | bytes accessed | tf_op | source)
XLA Modules:
  0.0 49.7 jit_solution(15782251268763301793)
XLA Ops:
  0.6 47.4 %exchange.1 = (f32[4,5,2,8192]{3,2,1,0:T(2,128)S(1)}, f32[16,8,128]{2,1,0:T(8,128)S(1)}) custom-call(bf16[5,24,8192]{2,1,0:T(8,128)(2,1)} %bitcast.5, f32[64,128]{1,0:T(8,128)} %bitcast.6, s32[32]{0:T(128)} %indices.1), custom_call_target="tpu_custom_call" | custom-call | tf_op jit(solution)/shard_map/exchange/pallas_call | solution.py:233
  48.0 1.7 %finish.1 = (f32[4,5,2,8192]{3,2,1,0:T(2,128)}, f32[2,2,2,2]{3,2,1,0:T(2,128)}) custom-call(f32[4,5,2,8192]{3,2,1,0:T(2,128)S(1)} %get-tuple-element.6.spectra, f32[16,8,128]{2,1,0:T(8,128)S(1)} %get-tuple-element.7.gram_in), custom_call_target="tpu_custom_call" | custom-call | tf_op jit(solution)/shard_map/finish/pallas_call | solution.py:272

commit v3 on v2

v3 whole, which is shorter than its diff:
```python
import functools
import math

import jax
import jax.numpy as jnp
from jax import lax
from jax.experimental import pallas as pl
from jax.experimental.pallas import tpu as pltpu
from jax.sharding import PartitionSpec as P

VARS = 5
BLK = 256
HOP = 128
SEGMENT_NUMBER = 2
RECORD_LENGTH = 384
RETAINED_MODES = 32
ROWS = RETAINED_MODES * SEGMENT_NUMBER * 2
MESH = pl.DeviceIdType.MESH
LANES = 128
STEPS = (
    (0, 1), (0, 3), (1, 0), (3, 0), (0, 2), (2, 0), (1, 1), (3, 3),
    (1, 3), (3, 1), (2, 1), (2, 3), (1, 2), (3, 2), (2, 2),
)
NEAR, SECOND, THIRD = slice(0, 4), slice(4, 10), slice(10, 14)


def cosine(phase):
    k = jnp.bitwise_and(phase, BLK - 1)
    k = jnp.where(k > BLK // 2, BLK - k, k)
    far = k > BLK // 4
    k = jnp.where(far, BLK // 2 - k, k)
    a = k.astype(jnp.float32) * jnp.float32(2.0 * math.pi / BLK)
    s = a * a
    total = jnp.float32(1.0 / math.factorial(12))
    for n in (10, 8, 6, 4, 2, 0):
        total = total * s * -1.0 if n == 10 else total * s
        total = total + jnp.float32((-1.0) ** (n // 2) / math.factorial(n))
    return jnp.where(far, -total, total)


def exchange_kernel(
    groups, width, cores, depth,
    snap, weights, indices, spectra, gram_out,
    mine, arrived, multipliers, twiddles, terms, turned, staged, held, w_ref, roots, idx_ref, sums, gram_mine, gram_seen, gram_sum,
    load_sem, own_sem, small_sem, send_sem, recv_sem, send_two, recv_two, gram_send, gram_recv, last_send, last_recv, known, here, everyone,
):
    me = lax.axis_index("ta")
    px, py = lax.axis_index("px"), lax.axis_index("py")
    side = math.isqrt(groups)
    y, x = me // side, me % side
    peers = [lax.rem(y + dy, side) * side + lax.rem(x + dx, side) for dy, dx in STEPS]
    place = px * depth + py
    others = [(dp, dz) for dz in range(depth) for dp in range(cores) if (dp, dz) != (0, 0)]
    planes = [(lax.rem(px + dp, cores), lax.rem(py + dz, depth)) for dp, dz in others]
    n, n_planes, tiles = len(peers), len(planes), width // LANES

    index_copy = pltpu.make_async_copy(indices, idx_ref, small_sem.at[0])
    index_copy.start()
    weight_copy = pltpu.make_async_copy(weights, w_ref, small_sem.at[1])
    weight_copy.start()
    loads = [pltpu.make_async_copy(snap.at[v], mine.at[v], load_sem.at[v]) for v in range(VARS)]
    for load in loads:
        load.start()
    own = pl.ds(pl.multiple_of(me * width, LANES), width)
    for v in range(VARS):
        pltpu.make_async_copy(snap.at[v, :, own], arrived.at[v, me], own_sem.at[v]).start()

    barrier = pltpu.get_barrier_semaphore()
    for peer in peers[NEAR]:
        pl.semaphore_signal(barrier, inc=1, device_id={"ta": peer}, device_id_type=MESH)

    @pl.when(place == 0)
    def _():
        for p, z in planes:
            pl.semaphore_signal(barrier, inc=1, device_id={"px": p, "py": z}, device_id_type=MESH)

    pl.semaphore_wait(barrier, jnp.where(place == 0, 4, 5))

    def tell(i):
        for peer in peers[NEAR]:
            pl.semaphore_signal(known.at[i], inc=1, device_id={"ta": peer}, device_id_type=MESH)

    def send(v, to):
        for peer in to:
            cut = pl.ds(pl.multiple_of(peer * width, LANES), width)
            pltpu.make_async_remote_copy(
                src_ref=mine.at[v, :, cut], dst_ref=arrived.at[v, me], send_sem=send_sem.at[v], recv_sem=recv_sem.at[v],
                device_id={"ta": peer}, device_id_type=MESH,
            ).start()

    def send_each(to):
        def step(v, carry):
            send(v, to)
            return carry

        return step

    tell(0)

    @pl.when(place != 0)
    def _():
        pl.semaphore_signal(here, inc=1, device_id={"px": 0, "py": 0}, device_id_type=MESH)

    for load in loads:
        load.wait()
    lax.fori_loop(0, VARS, send_each(peers[NEAR]), 0)
    pl.semaphore_wait(known.at[0], 4)
    tell(1)
    lax.fori_loop(0, VARS, send_each(peers[SECOND]), 0)
    pl.semaphore_wait(known.at[1], 4)
    tell(2)
    send(0, peers[THIRD])
    pl.semaphore_wait(known.at[2], 4)
    send(0, peers[14:])
    lax.fori_loop(1, VARS, send_each(peers[10:]), 0)

    index_copy.wait()
    shape = (8, RECORD_LENGTH)
    row = lax.broadcasted_iota(jnp.int32, shape, 0)
    time = lax.broadcasted_iota(jnp.int32, shape, 1)
    windows = []
    for b in range(SEGMENT_NUMBER):
        lag = time - HOP * b
        window = jnp.float32(0.5) - jnp.float32(0.5) * cosine(lag)
        window = jnp.where((lag >= 0) & (lag < BLK), window, jnp.float32(0.0))
        windows.append(window / jnp.sqrt(jnp.float32(3.0 * BLK / 8.0)))

    def fill(g, carry):
        index = jnp.full(shape, idx_ref[8 * g], jnp.int32)
        for i in range(1, 8):
            index = jnp.where(row == i, idx_ref[8 * g + i], index)
        for b in range(SEGMENT_NUMBER):
            phase = index * (time - HOP * b)
            for c in range(2):
                rows = pl.ds(pl.multiple_of(64 * c + 32 * b + 8 * g, 8), 8)
                multipliers[rows, :] = cosine(phase + (BLK // 4) * c) * windows[b]
        return carry

    lax.fori_loop(0, RETAINED_MODES // 8, fill, 0)
    twiddles[...] = multipliers[...].astype(jnp.bfloat16)
    sums[...] = jnp.zeros_like(sums)
    weight_copy.wait()
    root = jnp.sqrt(w_ref[...])
    for c in range(2):
        roots[pl.ds(c, groups * tiles, stride=2), :] = root

    @pl.when(place == 0)
    def _():
        pl.semaphore_wait(here, n_planes)
        for p, z in planes:
            pl.semaphore_signal(everyone, inc=1, device_id={"px": p, "py": z}, device_id_type=MESH)

    def transform(v):
        pltpu.make_async_copy(arrived.at[v, pl.ds(0, n)], arrived.at[v, pl.ds(0, n)], recv_sem.at[v]).wait()
        pltpu.make_async_copy(snap.at[v, :, own], arrived.at[v, me], own_sem.at[v]).wait()
        series = arrived[v].reshape(RECORD_LENGTH, width)
        raw = jnp.dot(twiddles[...], series, preferred_element_type=jnp.float32)
        terms[...] = raw
        for j in range(tiles):
            for b in range(SEGMENT_NUMBER):
                for c in range(2):
                    first = 64 * c + 32 * b
                    part = raw[first : first + RETAINED_MODES, j * LANES : (j + 1) * LANES]
                    turned[pl.ds(8 * b + 2 * j + c, RETAINED_MODES, stride=16), :] = part
        staged[v] = turned[...].astype(jnp.bfloat16).reshape(groups, 4, 8, LANES)
        held[v, me] = staged[v, me]
        total = [sums[i] for i in range(4)]
        for j in range(tiles):
            w = w_ref[pl.ds(me * tiles + j, 1), :]
            cut = slice(j * LANES, (j + 1) * LANES)
            r0, r1, i0, i1 = (terms[32 * i : 32 * i + 32, cut] for i in range(4))
            total[0] += (r0 * r0 + i0 * i0) * w
            total[1] += (r1 * r1 + i1 * i1) * w
            total[2] += (r0 * r1 + i0 * i1) * w
            total[3] += (r0 * i1 - i0 * r1) * w
        for i in range(4):
            sums[i] = total[i]

    def send_back(v):
        for peer in peers:
            pltpu.make_async_remote_copy(
                src_ref=staged.at[v, peer], dst_ref=held.at[v, me], send_sem=send_two.at[v], recv_sem=recv_two.at[v],
                device_id={"ta": peer}, device_id_type=MESH,
            ).start()

    def work(v, carry):
        transform(v)
        send_back(v)
        return carry

    lax.fori_loop(0, VARS - 1, work, 0)
    transform(VARS - 1)

    line = lax.broadcasted_iota(jnp.int32, (8, LANES), 0)
    shape = (RETAINED_MODES, LANES)
    diagonal = lax.broadcasted_iota(jnp.int32, shape, 0) == lax.broadcasted_iota(jnp.int32, shape, 1)
    both = jnp.zeros((8, LANES), jnp.float32)
    for i in range(4):
        column = jnp.sum(sums[i], axis=1, keepdims=True)
        lanes = jnp.sum(jnp.where(diagonal, column, jnp.float32(0.0)), axis=0, keepdims=True)
        both = jnp.where(line == i, lanes, both)
    gram_mine[...] = both

    @pl.when(place != 0)
    def _():
        pl.semaphore_wait(everyone, 1)

    gram_seen[place] = both
    for p, z in planes:
        pltpu.make_async_remote_copy(
            src_ref=gram_mine, dst_ref=gram_seen.at[place], send_sem=gram_send, recv_sem=gram_recv,
            device_id={"px": p, "py": z}, device_id_type=MESH,
        ).start()
    send_back(VARS - 1)

    def scale(v, carry):
        pltpu.make_async_copy(held.at[v, pl.ds(0, n)], held.at[v, pl.ds(0, n)], recv_two.at[v]).wait()
        for k in range(groups):
            by = roots[8 * k : 8 * k + 8, :]
            for i in range(4):
                spectra[i, v, k] = held[v, k, i].astype(jnp.float32) * by
        return carry

    lax.fori_loop(0, 2, scale, 0)
    pltpu.make_async_copy(gram_seen.at[pl.ds(0, n_planes)], gram_seen.at[pl.ds(0, n_planes)], gram_recv).wait()
    whole = jnp.sum(gram_seen[...], axis=0)
    gram_sum[...] = whole
    gram_out[me] = whole
    for peer in peers:
        pltpu.make_async_remote_copy(
            src_ref=gram_sum, dst_ref=gram_out.at[me], send_sem=last_send, recv_sem=last_recv,
            device_id={"ta": peer}, device_id_type=MESH,
        ).start()
    lax.fori_loop(2, VARS, scale, 0)
    pltpu.make_async_copy(gram_out.at[pl.ds(0, n)], gram_out.at[pl.ds(0, n)], last_recv).wait()
    for v in range(VARS):
        pltpu.make_async_copy(arrived.at[v, pl.ds(0, n)], arrived.at[v, pl.ds(0, n)], send_sem.at[v]).wait()
        pltpu.make_async_copy(held.at[v, pl.ds(0, n)], held.at[v, pl.ds(0, n)], send_two.at[v]).wait()
    pltpu.make_async_copy(gram_seen.at[pl.ds(0, n_planes)], gram_seen.at[pl.ds(0, n_planes)], gram_send).wait()
    pltpu.make_async_copy(gram_out.at[pl.ds(0, n)], gram_out.at[pl.ds(0, n)], last_send).wait()


def finish_kernel(total, spectra, gram_in, out, gram, sem):
    copies = [pltpu.make_async_copy(spectra.at[i], out.at[i], sem.at[i]) for i in range(4)]
    for copy in copies:
        copy.start()
    me = lax.axis_index("ta")
    sums = jnp.sum(gram_in[...], axis=0) / jnp.float32(total)
    sums = pltpu.roll(sums, lax.rem(LANES - 2 * me, LANES), 1)
    r = lax.broadcasted_iota(jnp.int32, (2, 2), 0)
    c = lax.broadcasted_iota(jnp.int32, (2, 2), 1)
    zero = jnp.zeros((2, 2), jnp.float32)
    for f in range(2):
        first, second, real, imag = (jnp.broadcast_to(sums[i : i + 1, f : f + 1], (2, 2)) for i in range(4))
        for b in range(2):
            power = jnp.where(c == 0, second if b else first, zero)
            gram[f, b] = jnp.where(r == b, power, jnp.where(c == 0, real, -imag if b else imag))
    for copy in copies:
        copy.wait()


def solution(mesh):
    groups, cores, depth = mesh.shape["ta"], mesh.shape["px"], mesh.shape["py"]

    def on_device(snapshots, quad_weights, spectral_indices):
        steps, _, points = snapshots.shape
        width = points // groups
        series = jnp.transpose(snapshots, (1, 0, 2))
        weights = quad_weights.reshape(points // LANES, LANES)
        hbm = pl.BlockSpec(memory_space=pltpu.HBM)
        vmem = pl.BlockSpec(memory_space=pltpu.VMEM)
        spectra, gram_parts = pl.pallas_call(
            functools.partial(exchange_kernel, groups, width, cores, depth),
            name="exchange",
            out_shape=(
                jax.ShapeDtypeStruct((4, VARS, groups, 8, LANES), jnp.float32),
                jax.ShapeDtypeStruct((groups, 8, LANES), jnp.float32),
            ),
            in_specs=[hbm, hbm, hbm],
            out_specs=(vmem, vmem),
            scratch_shapes=[
                pltpu.VMEM((VARS, steps, points), jnp.bfloat16),
                pltpu.VMEM((VARS, groups, steps, width), jnp.bfloat16),
                pltpu.VMEM((ROWS, RECORD_LENGTH), jnp.float32),
                pltpu.VMEM((ROWS, RECORD_LENGTH), jnp.bfloat16),
                pltpu.VMEM((ROWS, width), jnp.float32),
                pltpu.VMEM((ROWS * width // LANES, LANES), jnp.float32),
                pltpu.VMEM((VARS, groups, 4, 8, LANES), jnp.bfloat16),
                pltpu.VMEM((VARS, groups, 4, 8, LANES), jnp.bfloat16),
                pltpu.VMEM((points // LANES, LANES), jnp.float32),
                pltpu.VMEM((2 * points // LANES, LANES), jnp.float32),
                pltpu.SMEM((RETAINED_MODES,), jnp.int32),
                pltpu.VMEM((4, RETAINED_MODES, LANES), jnp.float32),
                pltpu.VMEM((8, LANES), jnp.float32),
                pltpu.VMEM((cores * depth, 8, LANES), jnp.float32),
                pltpu.VMEM((8, LANES), jnp.float32),
                pltpu.SemaphoreType.DMA((VARS,)),
                pltpu.SemaphoreType.DMA((VARS,)),
                pltpu.SemaphoreType.DMA((2,)),
                pltpu.SemaphoreType.DMA((VARS,)),
                pltpu.SemaphoreType.DMA((VARS,)),
                pltpu.SemaphoreType.DMA((VARS,)),
                pltpu.SemaphoreType.DMA((VARS,)),
                pltpu.SemaphoreType.DMA,
                pltpu.SemaphoreType.DMA,
                pltpu.SemaphoreType.DMA,
                pltpu.SemaphoreType.DMA,
                pltpu.SemaphoreType.REGULAR((3,)),
                pltpu.SemaphoreType.REGULAR,
                pltpu.SemaphoreType.REGULAR,
            ],
            compiler_params=pltpu.CompilerParams(collective_id=0, has_side_effects=True, vmem_limit_bytes=32 * 2**20),
        )(*(pltpu.with_memory_space_constraint(a, pltpu.HBM) for a in (series, weights, spectral_indices)))
        total = points * cores * depth * VARS
        spectra, gram = pl.pallas_call(
            functools.partial(finish_kernel, total),
            name="finish",
            out_shape=(
                jax.ShapeDtypeStruct((4, VARS, groups, 8, LANES), jnp.float32),
                jax.ShapeDtypeStruct((2, 2, 2, 2), jnp.float32),
            ),
            in_specs=[vmem, vmem],
            out_specs=(hbm, vmem),
            scratch_shapes=[pltpu.SemaphoreType.DMA((4,))],
            compiler_params=pltpu.CompilerParams(vmem_limit_bytes=8 * 2**20),
        )(spectra, gram_parts)
        spectra = spectra.reshape(2, SEGMENT_NUMBER, VARS, groups, width // LANES, 2, LANES)
        spectra = spectra.transpose(0, 1, 5, 2, 3, 4, 6).reshape(2, SEGMENT_NUMBER, 2, VARS, points)
        return (spectra, gram)

    return jax.shard_map(
        on_device,
        mesh=mesh,
        in_specs=(P("ta", None, ("px", "py")), P(("px", "py")), P()),
        out_specs=(P("ta", None, None, None, ("px", "py")), P("ta", None, None, None)),
        check_vma=False,
    )
```

time: 49.8 us -> 47.4 us (0.952)
  Pallas kernels: 49 us -> 46.6 us
    pallas_call x1, Pallas kernels: 47.4 us -> 45 us  [on_device(): pl.pallas_call(functools.partial(exchange_kernel, groups, width, cores, d...]
where the time goes in v3:
time: 47.4 us; the launch traced here: 47.3 us
  Pallas kernels  46.6 us (98%)
  between operations  0.64 us (1%)
    pallas_call x1, Pallas kernels, on_device(): pl.pallas_call(functools.partial(exchange_kernel, groups, width, cores, d...  45 us
    pallas_call x1, Pallas kernels, on_device(): pl.pallas_call(functools.partial(finish_kernel, total), name='finish', ou...  1.68 us

profile of v3, /device:TPU:1, one launch (start us, length us, event | category | flops | bytes accessed | tf_op | source)
XLA Modules:
  0.0 47.3 jit_solution(16548265333918232476)
XLA Ops:
  0.6 45.0 %exchange.1 = (f32[4,5,16,8,128]{4,3,2,1,0:T(8,128)S(1)}, f32[16,8,128]{2,1,0:T(8,128)S(1)}) custom-call(bf16[5,24,8192]{2,1,0:T(8,128)(2,1)} %bitcast.7, f32[64,128]{1,0:T(8,128)} %bitcast.8, s32[32]{0:T(128)} %indices.1), custom_call_target="tpu_custom_call" | custom-call | tf_op jit(solution)/shard_map/exchange/pallas_call | solution.py:272
  45.6 1.7 %finish.1 = (f32[4,5,16,8,128]{4,3,2,1,0:T(8,128)}, f32[2,2,2,2]{3,2,1,0:T(2,128)}) custom-call(f32[4,5,16,8,128]{4,3,2,1,0:T(8,128)S(1)} %get-tuple-element.6.spectra, f32[16,8,128]{2,1,0:T(8,128)S(1)} %get-tuple-element.7.gram_in), custom_call_target="tpu_custom_call" | custom-call | tf_op jit(solution)/shard_map/finish/pallas_call | solution.py:315

commit v4 on v3

--- a/solution.py
+++ b/solution.py
@@ -52,27 +52,28 @@
     place = px * depth + py
     others = [(dp, dz) for dz in range(depth) for dp in range(cores) if (dp, dz) != (0, 0)]
     planes = [(lax.rem(px + dp, cores), lax.rem(py + dz, depth)) for dp, dz in others]
+    far_planes = [planes[i] for i in sorted(range(len(others)), key=lambda i: -min(others[i][1], depth - others[i][1]))]
     n, n_planes, tiles = len(peers), len(planes), width // LANES
 
+    barrier = pltpu.get_barrier_semaphore()
+    for peer in peers[NEAR]:
+        pl.semaphore_signal(barrier, inc=1, device_id={"ta": peer}, device_id_type=MESH)
+
+    @pl.when(place == 0)
+    def _():
+        for p, z in planes:
+            pl.semaphore_signal(barrier, inc=1, device_id={"px": p, "py": z}, device_id_type=MESH)
+
+    loads = [pltpu.make_async_copy(snap.at[v], mine.at[v], load_sem.at[v]) for v in range(VARS)]
+    for load in loads:
+        load.start()
     index_copy = pltpu.make_async_copy(indices, idx_ref, small_sem.at[0])
     index_copy.start()
     weight_copy = pltpu.make_async_copy(weights, w_ref, small_sem.at[1])
     weight_copy.start()
-    loads = [pltpu.make_async_copy(snap.at[v], mine.at[v], load_sem.at[v]) for v in range(VARS)]
-    for load in loads:
-        load.start()
     own = pl.ds(pl.multiple_of(me * width, LANES), width)
     for v in range(VARS):
         pltpu.make_async_copy(snap.at[v, :, own], arrived.at[v, me], own_sem.at[v]).start()
-
-    barrier = pltpu.get_barrier_semaphore()
-    for peer in peers[NEAR]:
-        pl.semaphore_signal(barrier, inc=1, device_id={"ta": peer}, device_id_type=MESH)
-
-    @pl.when(place == 0)
-    def _():
-        for p, z in planes:
-            pl.semaphore_signal(barrier, inc=1, device_id={"px": p, "py": z}, device_id_type=MESH)
 
     pl.semaphore_wait(barrier, jnp.where(place == 0, 4, 5))
 
@@ -101,18 +102,20 @@
     def _():
         pl.semaphore_signal(here, inc=1, device_id={"px": 0, "py": 0}, device_id_type=MESH)
 
-    for load in loads:
-        load.wait()
-    lax.fori_loop(0, VARS, send_each(peers[NEAR]), 0)
+    for v in range(VARS - 1):
+        loads[v].wait()
+        send(v, peers[NEAR])
+    loads[VARS - 1].wait()
     pl.semaphore_wait(known.at[0], 4)
     tell(1)
-    lax.fori_loop(0, VARS, send_each(peers[SECOND]), 0)
+    lax.fori_loop(0, VARS - 1, send_each(peers[SECOND]), 0)
     pl.semaphore_wait(known.at[1], 4)
     tell(2)
     send(0, peers[THIRD])
     pl.semaphore_wait(known.at[2], 4)
     send(0, peers[14:])
-    lax.fori_loop(1, VARS, send_each(peers[10:]), 0)
+    lax.fori_loop(1, VARS - 1, send_each(peers[10:]), 0)
+    send(VARS - 1, peers[::-1])
 
     index_copy.wait()
     shape = (8, RECORD_LENGTH)
@@ -156,14 +159,6 @@
         series = arrived[v].reshape(RECORD_LENGTH, width)
         raw = jnp.dot(twiddles[...], series, preferred_element_type=jnp.float32)
         terms[...] = raw
-        for j in range(tiles):
-            for b in range(SEGMENT_NUMBER):
-                for c in range(2):
-                    first = 64 * c + 32 * b
-                    part = raw[first : first + RETAINED_MODES, j * LANES : (j + 1) * LANES]
-                    turned[pl.ds(8 * b + 2 * j + c, RETAINED_MODES, stride=16), :] = part
-        staged[v] = turned[...].astype(jnp.bfloat16).reshape(groups, 4, 8, LANES)
-        held[v, me] = staged[v, me]
         total = [sums[i] for i in range(4)]
         for j in range(tiles):
             w = w_ref[pl.ds(me * tiles + j, 1), :]
@@ -176,8 +171,18 @@
         for i in range(4):
             sums[i] = total[i]
 
+    def lay_out(v):
+        for j in range(tiles):
+            for b in range(SEGMENT_NUMBER):
+                for c in range(2):
+                    first = 64 * c + 32 * b
+                    part = terms[first : first + RETAINED_MODES, j * LANES : (j + 1) * LANES]
+                    turned[pl.ds(8 * b + 2 * j + c, RETAINED_MODES, stride=16), :] = part
+        staged[v] = turned[...].astype(jnp.bfloat16).reshape(groups, 4, 8, LANES)
+        held[v, me] = staged[v, me]
+
     def send_back(v):
-        for peer in peers:
+        for peer in peers[::-1]:
             pltpu.make_async_remote_copy(
                 src_ref=staged.at[v, peer], dst_ref=held.at[v, me], send_sem=send_two.at[v], recv_sem=recv_two.at[v],
                 device_id={"ta": peer}, device_id_type=MESH,
@@ -185,32 +190,36 @@
 
     def work(v, carry):
         transform(v)
-        send_back(v)
+        lay_out(v)
         return carry
 
     lax.fori_loop(0, VARS - 1, work, 0)
     transform(VARS - 1)
 
-    line = lax.broadcasted_iota(jnp.int32, (8, LANES), 0)
     shape = (RETAINED_MODES, LANES)
-    diagonal = lax.broadcasted_iota(jnp.int32, shape, 0) == lax.broadcasted_iota(jnp.int32, shape, 1)
-    both = jnp.zeros((8, LANES), jnp.float32)
+    ahead = lax.broadcasted_iota(jnp.int32, shape, 1) - lax.broadcasted_iota(jnp.int32, shape, 0)
+    lanes = jnp.zeros(shape, jnp.float32)
     for i in range(4):
-        column = jnp.sum(sums[i], axis=1, keepdims=True)
-        lanes = jnp.sum(jnp.where(diagonal, column, jnp.float32(0.0)), axis=0, keepdims=True)
-        both = jnp.where(line == i, lanes, both)
-    gram_mine[...] = both
+        lanes = jnp.where(ahead == RETAINED_MODES * i, jnp.sum(sums[i], axis=1, keepdims=True), lanes)
+    lanes = jnp.sum(lanes, axis=0, keepdims=True)
+    gram_mine[...] = lanes
+    gram_seen[place] = lanes
 
     @pl.when(place != 0)
     def _():
         pl.semaphore_wait(everyone, 1)
 
-    gram_seen[place] = both
-    for p, z in planes:
+    for p, z in far_planes:
         pltpu.make_async_remote_copy(
             src_ref=gram_mine, dst_ref=gram_seen.at[place], send_sem=gram_send, recv_sem=gram_recv,
             device_id={"px": p, "py": z}, device_id_type=MESH,
         ).start()
+    def send_early(v, carry):
+        send_back(v)
+        return carry
+
+    lax.fori_loop(0, VARS - 1, send_early, 0)
+    lay_out(VARS - 1)
     send_back(VARS - 1)
 
     def scale(v, carry):
@@ -226,7 +235,7 @@
     whole = jnp.sum(gram_seen[...], axis=0)
     gram_sum[...] = whole
     gram_out[me] = whole
-    for peer in peers:
+    for peer in peers[::-1]:
         pltpu.make_async_remote_copy(
             src_ref=gram_sum, dst_ref=gram_out.at[me], send_sem=last_send, recv_sem=last_recv,
             device_id={"ta": peer}, device_id_type=MESH,
@@ -240,7 +249,7 @@
     pltpu.make_async_copy(gram_out.at[pl.ds(0, n)], gram_out.at[pl.ds(0, n)], last_send).wait()
 
 
-def finish_kernel(total, spectra, gram_in, out, gram, sem):
+def finish_kernel(total, spectra, gram_in, out, gram_out, gram, sem):
     copies = [pltpu.make_async_copy(spectra.at[i], out.at[i], sem.at[i]) for i in range(4)]
     for copy in copies:
         copy.start()
@@ -251,10 +260,12 @@
     c = lax.broadcasted_iota(jnp.int32, (2, 2), 1)
     zero = jnp.zeros((2, 2), jnp.float32)
     for f in range(2):
-        first, second, real, imag = (jnp.broadcast_to(sums[i : i + 1, f : f + 1], (2, 2)) for i in range(4))
+        first, second, real, imag = (jnp.broadcast_to(sums[:, RETAINED_MODES * i + f : RETAINED_MODES * i + f + 1], (2, 2)) for i in range(4))
         for b in range(2):
             power = jnp.where(c == 0, second if b else first, zero)
             gram[f, b] = jnp.where(r == b, power, jnp.where(c == 0, real, -imag if b else imag))
+    copies.append(pltpu.make_async_copy(gram, gram_out, sem.at[4]))
+    copies[-1].start()
     for copy in copies:
         copy.wait()
 
@@ -274,7 +285,7 @@
             name="exchange",
             out_shape=(
                 jax.ShapeDtypeStruct((4, VARS, groups, 8, LANES), jnp.float32),
-                jax.ShapeDtypeStruct((groups, 8, LANES), jnp.float32),
+                jax.ShapeDtypeStruct((groups, 1, LANES), jnp.float32),
             ),
             in_specs=[hbm, hbm, hbm],
             out_specs=(vmem, vmem),
@@ -291,9 +302,9 @@
                 pltpu.VMEM((2 * points // LANES, LANES), jnp.float32),
                 pltpu.SMEM((RETAINED_MODES,), jnp.int32),
                 pltpu.VMEM((4, RETAINED_MODES, LANES), jnp.float32),
-                pltpu.VMEM((8, LANES), jnp.float32),
-                pltpu.VMEM((cores * depth, 8, LANES), jnp.float32),
-                pltpu.VMEM((8, LANES), jnp.float32),
+                pltpu.VMEM((1, LANES), jnp.float32),
+                pltpu.VMEM((cores * depth, 1, LANES), jnp.float32),
+                pltpu.VMEM((1, LANES), jnp.float32),
                 pltpu.SemaphoreType.DMA((VARS,)),
                 pltpu.SemaphoreType.DMA((VARS,)),
                 pltpu.SemaphoreType.DMA((2,)),
@@ -320,8 +331,8 @@
                 jax.ShapeDtypeStruct((2, 2, 2, 2), jnp.float32),
             ),
             in_specs=[vmem, vmem],
-            out_specs=(hbm, vmem),
-            scratch_shapes=[pltpu.SemaphoreType.DMA((4,))],
+            out_specs=(hbm, hbm),
+            scratch_shapes=[pltpu.VMEM((2, 2, 2, 2), jnp.float32), pltpu.SemaphoreType.DMA((5,))],
             compiler_params=pltpu.CompilerParams(vmem_limit_bytes=8 * 2**20),
         )(spectra, gram_parts)
         spectra = spectra.reshape(2, SEGMENT_NUMBER, VARS, groups, width // LANES, 2, LANES)

time: 47.4 us -> 43.7 us (0.922)
  Pallas kernels: 46.6 us -> 43 us
    pallas_call x1, Pallas kernels: 45 us -> 41.9 us  [on_device(): pl.pallas_call(functools.partial(exchange_kernel, groups, width, cores, d...]
    pallas_call x1, Pallas kernels: 1.68 us -> 1.1 us  [on_device(): pl.pallas_call(functools.partial(finish_kernel, total), name='finish', ou...]
where the time goes in v4:
time: 43.7 us; the launch traced here: 43.6 us
  Pallas kernels  43 us (98%)
  between operations  0.64 us (1%)
    pallas_call x1, Pallas kernels, on_device(): pl.pallas_call(functools.partial(exchange_kernel, groups, width, cores, d...  41.9 us
    pallas_call x1, Pallas kernels, on_device(): pl.pallas_call(functools.partial(finish_kernel, total), name='finish', ou...  1.1 us

profile of v4, /device:TPU:1, one launch (start us, length us, event | category | flops | bytes accessed | tf_op | source)
XLA Modules:
  0.0 43.6 jit_solution(4381683291248082187)
XLA Ops:
  0.6 41.9 %exchange.1 = (f32[4,5,16,8,128]{4,3,2,1,0:T(8,128)S(1)}, f32[16,1,128]{2,1,0:T(1,128)S(1)}) custom-call(bf16[5,24,8192]{2,1,0:T(8,128)(2,1)} %bitcast.7, f32[64,128]{1,0:T(8,128)} %bitcast.8, s32[32]{0:T(128)} %indices.1), custom_call_target="tpu_custom_call" | custom-call | tf_op jit(solution)/shard_map/exchange/pallas_call | solution.py:283
  42.5 1.1 %finish.1 = (f32[4,5,16,8,128]{4,3,2,1,0:T(8,128)}, f32[2,2,2,2]{3,2,1,0:T(2,128)}) custom-call(f32[4,5,16,8,128]{4,3,2,1,0:T(8,128)S(1)} %get-tuple-element.6.spectra, f32[16,1,128]{2,1,0:T(1,128)S(1)} %get-tuple-element.7.gram_in), custom_call_target="tpu_custom_call" | custom-call | tf_op jit(solution)/shard_map/finish/pallas_call | solution.py:326

commit v5 on v4

--- a/solution.py
+++ b/solution.py
@@ -17,6 +17,7 @@
 ROWS = RETAINED_MODES * SEGMENT_NUMBER * 2
 MESH = pl.DeviceIdType.MESH
 LANES = 128
+BORROWED = 128
 STEPS = (
     (0, 1), (0, 3), (1, 0), (3, 0), (0, 2), (2, 0), (1, 1), (3, 3),
     (1, 3), (3, 1), (2, 1), (2, 3), (1, 2), (3, 2), (2, 2),
@@ -42,40 +43,66 @@
     groups, width, cores, depth,
     snap, weights, indices, spectra, gram_out,
     mine, arrived, multipliers, twiddles, terms, turned, staged, held, w_ref, roots, idx_ref, sums, gram_mine, gram_seen, gram_sum,
-    load_sem, own_sem, small_sem, send_sem, recv_sem, send_two, recv_two, gram_send, gram_recv, last_send, last_recv, known, here, everyone,
+    load_sem, own_sem, small_sem, send_sem, recv_sem, send_two, recv_two, gram_send, gram_recv, last_send, last_recv, known, here, everyone, relay, relay_sem,
 ):
     me = lax.axis_index("ta")
-    px, py = lax.axis_index("px"), lax.axis_index("py")
     side = math.isqrt(groups)
     y, x = me // side, me % side
-    peers = [lax.rem(y + dy, side) * side + lax.rem(x + dx, side) for dy, dx in STEPS]
+
+    def member(step):
+        return lax.rem(y + step[0], side) * side + lax.rem(x + step[1], side)
+
+    barrier = pltpu.get_barrier_semaphore()
+    peers = [member(step) for step in STEPS[NEAR]]
+    for peer in peers:
+        pl.semaphore_signal(barrier, inc=1, device_id={"ta": peer}, device_id_type=MESH)
+    loads = [pltpu.make_async_copy(snap.at[v], mine.at[v], load_sem.at[v]) for v in range(VARS)]
+    for load in loads:
+        load.start()
+    px, py = lax.axis_index("px"), lax.axis_index("py")
+    late, partner = py >= depth // 2, depth - 1 - py
+    last = VARS - 1
     place = px * depth + py
     others = [(dp, dz) for dz in range(depth) for dp in range(cores) if (dp, dz) != (0, 0)]
+
+    @pl.when(place == 0)
+    def _():
+        for p, z in others:
+            pl.semaphore_signal(barrier, inc=1, device_id={"px": p, "py": z}, device_id_type=MESH)
+
+    @pl.when(jnp.logical_not(late))
+    def _():
+        pl.semaphore_signal(barrier, inc=1, device_id={"py": partner}, device_id_type=MESH)
+
+    peers += [member(step) for step in STEPS[NEAR.stop :]]
     planes = [(lax.rem(px + dp, cores), lax.rem(py + dz, depth)) for dp, dz in others]
     far_planes = [planes[i] for i in sorted(range(len(others)), key=lambda i: -min(others[i][1], depth - others[i][1]))]
     n, n_planes, tiles = len(peers), len(planes), width // LANES
-
-    barrier = pltpu.get_barrier_semaphore()
-    for peer in peers[NEAR]:
-        pl.semaphore_signal(barrier, inc=1, device_id={"ta": peer}, device_id_type=MESH)
-
-    @pl.when(place == 0)
-    def _():
-        for p, z in planes:
-            pl.semaphore_signal(barrier, inc=1, device_id={"px": p, "py": z}, device_id_type=MESH)
-
-    loads = [pltpu.make_async_copy(snap.at[v], mine.at[v], load_sem.at[v]) for v in range(VARS)]
-    for load in loads:
-        load.start()
     index_copy = pltpu.make_async_copy(indices, idx_ref, small_sem.at[0])
     index_copy.start()
     weight_copy = pltpu.make_async_copy(weights, w_ref, small_sem.at[1])
     weight_copy.start()
     own = pl.ds(pl.multiple_of(me * width, LANES), width)
-    for v in range(VARS):
+    kept = pl.ds(BORROWED, width - BORROWED)
+    for v in range(last):
         pltpu.make_async_copy(snap.at[v, :, own], arrived.at[v, me], own_sem.at[v]).start()
 
-    pl.semaphore_wait(barrier, jnp.where(place == 0, 4, 5))
+    def own_last():
+        cut = pl.ds(pl.multiple_of(me * width + BORROWED, LANES), width - BORROWED)
+        return pltpu.make_async_copy(snap.at[last, :, cut], arrived.at[last, me, :, kept], own_sem.at[last])
+
+    def own_whole(v):
+        return pltpu.make_async_copy(snap.at[v, :, own], arrived.at[v, me], own_sem.at[v])
+
+    @pl.when(late)
+    def _():
+        own_last().start()
+
+    @pl.when(jnp.logical_not(late))
+    def _():
+        own_whole(last).start()
+
+    pl.semaphore_wait(barrier, jnp.where(place == 0, 4, jnp.where(late, 6, 5)))
 
     def tell(i):
         for peer in peers[NEAR]:
@@ -113,9 +140,34 @@
     tell(2)
     send(0, peers[THIRD])
     pl.semaphore_wait(known.at[2], 4)
+    tell(3)
     send(0, peers[14:])
+    pl.semaphore_wait(known.at[3], 4)
+
+    @pl.when(late)
+    def _():
+        for peer in [*peers[::-1], me]:
+            cut = pl.ds(pl.multiple_of(peer * width, LANES), BORROWED)
+            pltpu.make_async_remote_copy(
+                src_ref=mine.at[last, :, cut], dst_ref=relay.at[me], send_sem=relay_sem.at[0], recv_sem=relay_sem.at[1],
+                device_id={"ta": peer, "py": partner}, device_id_type=MESH,
+            ).start()
+
     lax.fori_loop(1, VARS - 1, send_each(peers[10:]), 0)
-    send(VARS - 1, peers[::-1])
+
+    @pl.when(late)
+    def _():
+        for peer in peers[::-1]:
+            cut = pl.ds(pl.multiple_of(peer * width + BORROWED, LANES), width - BORROWED)
+            pltpu.make_async_remote_copy(
+                src_ref=mine.at[last, :, cut], dst_ref=arrived.at[last, me, :, kept],
+                send_sem=send_sem.at[last], recv_sem=recv_sem.at[last],
+                device_id={"ta": peer}, device_id_type=MESH,
+            ).start()
+
+    @pl.when(jnp.logical_not(late))
+    def _():
+        send(last, peers[::-1])
 
     index_copy.wait()
     shape = (8, RECORD_LENGTH)
@@ -150,12 +202,17 @@
     @pl.when(place == 0)
     def _():
         pl.semaphore_wait(here, n_planes)
-        for p, z in planes:
+        for p, z in others:
             pl.semaphore_signal(everyone, inc=1, device_id={"px": p, "py": z}, device_id_type=MESH)
 
+    def arrive(v):
+        pltpu.make_async_copy(arrived.at[v, pl.ds(0, n)], arrived.at[v, pl.ds(0, n)], recv_sem.at[v]).wait()
+        own_whole(v).wait()
+
+    def parts_of_last():
+        return arrived.at[last, pl.ds(0, n), :, kept]
+
     def transform(v):
-        pltpu.make_async_copy(arrived.at[v, pl.ds(0, n)], arrived.at[v, pl.ds(0, n)], recv_sem.at[v]).wait()
-        pltpu.make_async_copy(snap.at[v, :, own], arrived.at[v, me], own_sem.at[v]).wait()
         series = arrived[v].reshape(RECORD_LENGTH, width)
         raw = jnp.dot(twiddles[...], series, preferred_element_type=jnp.float32)
         terms[...] = raw
@@ -189,12 +246,33 @@
             ).start()
 
     def work(v, carry):
+        arrive(v)
         transform(v)
         lay_out(v)
         return carry
 
+    @pl.when(jnp.logical_not(late))
+    def _():
+        pltpu.make_async_copy(relay, relay, relay_sem.at[1]).wait()
+        pltpu.make_async_remote_copy(
+            src_ref=relay, dst_ref=arrived.at[last, :, :, pl.ds(0, BORROWED)],
+            send_sem=relay_sem.at[2], recv_sem=relay_sem.at[3],
+            device_id={"py": partner}, device_id_type=MESH,
+        ).start()
+
     lax.fori_loop(0, VARS - 1, work, 0)
-    transform(VARS - 1)
+
+    @pl.when(late)
+    def _():
+        own_last().wait()
+        pltpu.make_async_copy(parts_of_last(), parts_of_last(), recv_sem.at[last]).wait()
+        pltpu.make_async_copy(relay, relay, relay_sem.at[3]).wait()
+
+    @pl.when(jnp.logical_not(late))
+    def _():
+        arrive(last)
+
+    transform(last)
 
     shape = (RETAINED_MODES, LANES)
     ahead = lax.broadcasted_iota(jnp.int32, shape, 1) - lax.broadcasted_iota(jnp.int32, shape, 0)
@@ -242,8 +320,20 @@
         ).start()
     lax.fori_loop(2, VARS, scale, 0)
     pltpu.make_async_copy(gram_out.at[pl.ds(0, n)], gram_out.at[pl.ds(0, n)], last_recv).wait()
+    for v in range(last):
+        pltpu.make_async_copy(arrived.at[v, pl.ds(0, n)], arrived.at[v, pl.ds(0, n)], send_sem.at[v]).wait()
+
+    @pl.when(late)
+    def _():
+        pltpu.make_async_copy(parts_of_last(), parts_of_last(), send_sem.at[last]).wait()
+        pltpu.make_async_copy(relay, relay, relay_sem.at[0]).wait()
+
+    @pl.when(jnp.logical_not(late))
+    def _():
+        pltpu.make_async_copy(arrived.at[last, pl.ds(0, n)], arrived.at[last, pl.ds(0, n)], send_sem.at[last]).wait()
+        pltpu.make_async_copy(relay, relay, relay_sem.at[2]).wait()
+
     for v in range(VARS):
-        pltpu.make_async_copy(arrived.at[v, pl.ds(0, n)], arrived.at[v, pl.ds(0, n)], send_sem.at[v]).wait()
         pltpu.make_async_copy(held.at[v, pl.ds(0, n)], held.at[v, pl.ds(0, n)], send_two.at[v]).wait()
     pltpu.make_async_copy(gram_seen.at[pl.ds(0, n_planes)], gram_seen.at[pl.ds(0, n_planes)], gram_send).wait()
     pltpu.make_async_copy(gram_out.at[pl.ds(0, n)], gram_out.at[pl.ds(0, n)], last_send).wait()
@@ -316,9 +406,11 @@
                 pltpu.SemaphoreType.DMA,
                 pltpu.SemaphoreType.DMA,
                 pltpu.SemaphoreType.DMA,
-                pltpu.SemaphoreType.REGULAR((3,)),
+                pltpu.SemaphoreType.REGULAR((4,)),
                 pltpu.SemaphoreType.REGULAR,
                 pltpu.SemaphoreType.REGULAR,
+                pltpu.VMEM((groups, steps, BORROWED), jnp.bfloat16),
+                pltpu.SemaphoreType.DMA((4,)),
             ],
             compiler_params=pltpu.CompilerParams(collective_id=0, has_side_effects=True, vmem_limit_bytes=32 * 2**20),
         )(*(pltpu.with_memory_space_constraint(a, pltpu.HBM) for a in (series, weights, spectral_indices)))

time: 43.7 us -> 42.6 us (0.975)
  Pallas kernels: 43 us -> 41.9 us
    pallas_call x1, Pallas kernels: 41.9 us -> 40.8 us  [on_device(): pl.pallas_call(functools.partial(exchange_kernel, groups, width, cores, d...]
where the time goes in v5:
time: 42.6 us; the launch traced here: 42.5 us
  Pallas kernels  41.9 us (98%)
  between operations  0.64 us (2%)
    pallas_call x1, Pallas kernels, on_device(): pl.pallas_call(functools.partial(exchange_kernel, groups, width, cores, d...  40.8 us
    pallas_call x1, Pallas kernels, on_device(): pl.pallas_call(functools.partial(finish_kernel, total), name='finish', ou...  1.1 us

profile of v5, /device:TPU:1, one launch (start us, length us, event | category | flops | bytes accessed | tf_op | source)
XLA Modules:
  0.0 42.5 jit_solution(9694896111229112705)
XLA Ops:
  0.6 40.8 %exchange.1 = (f32[4,5,16,8,128]{4,3,2,1,0:T(8,128)S(1)}, f32[16,1,128]{2,1,0:T(1,128)S(1)}) custom-call(bf16[5,24,8192]{2,1,0:T(8,128)(2,1)} %bitcast.7, f32[64,128]{1,0:T(8,128)} %bitcast.8, s32[32]{0:T(128)} %indices.1), custom_call_target="tpu_custom_call" | custom-call | tf_op jit(solution)/shard_map/exchange/pallas_call | solution.py:373
  41.4 1.1 %finish.1 = (f32[4,5,16,8,128]{4,3,2,1,0:T(8,128)}, f32[2,2,2,2]{3,2,1,0:T(2,128)}) custom-call(f32[4,5,16,8,128]{4,3,2,1,0:T(8,128)S(1)} %get-tuple-element.6.spectra, f32[16,1,128]{2,1,0:T(1,128)S(1)} %get-tuple-element.7.gram_in), custom_call_target="tpu_custom_call" | custom-call | tf_op jit(solution)/shard_map/finish/pallas_call | solution.py:418

commit v6 on v5

--- a/solution.py
+++ b/solution.py
@@ -220,7 +220,7 @@
         for j in range(tiles):
             w = w_ref[pl.ds(me * tiles + j, 1), :]
             cut = slice(j * LANES, (j + 1) * LANES)
-            r0, r1, i0, i1 = (terms[32 * i : 32 * i + 32, cut] for i in range(4))
+            r0, r1, i0, i1 = (raw[32 * i : 32 * i + 32, cut] for i in range(4))
             total[0] += (r0 * r0 + i0 * i0) * w
             total[1] += (r1 * r1 + i1 * i1) * w
             total[2] += (r0 * r1 + i0 * i1) * w
@@ -292,13 +292,13 @@
             src_ref=gram_mine, dst_ref=gram_seen.at[place], send_sem=gram_send, recv_sem=gram_recv,
             device_id={"px": p, "py": z}, device_id_type=MESH,
         ).start()
-    def send_early(v, carry):
+    lay_out(last)
+
+    def send_in_turn(v, carry):
         send_back(v)
         return carry
 
-    lax.fori_loop(0, VARS - 1, send_early, 0)
-    lay_out(VARS - 1)
-    send_back(VARS - 1)
+    lax.fori_loop(0, VARS, send_in_turn, 0)
 
     def scale(v, carry):
         pltpu.make_async_copy(held.at[v, pl.ds(0, n)], held.at[v, pl.ds(0, n)], recv_two.at[v]).wait()

time: 42.6 us -> 42.7 us (level)
  no operation moved by 1% of the time
where the time goes in v6:
time: 42.7 us; the launch traced here: 42.6 us
  Pallas kernels  42 us (98%)
  between operations  0.64 us (1%)
    pallas_call x1, Pallas kernels, on_device(): pl.pallas_call(functools.partial(exchange_kernel, groups, width, cores, d...  40.9 us
    pallas_call x1, Pallas kernels, on_device(): pl.pallas_call(functools.partial(finish_kernel, total), name='finish', ou...  1.1 us

profile of v6, /device:TPU:1, one launch (start us, length us, event | category | flops | bytes accessed | tf_op | source)
XLA Modules:
  0.0 42.6 jit_solution(3310687585495285723)
XLA Ops:
  0.6 40.9 %exchange.1 = (f32[4,5,16,8,128]{4,3,2,1,0:T(8,128)S(1)}, f32[16,1,128]{2,1,0:T(1,128)S(1)}) custom-call(bf16[5,24,8192]{2,1,0:T(8,128)(2,1)} %bitcast.7, f32[64,128]{1,0:T(8,128)} %bitcast.8, s32[32]{0:T(128)} %indices.1), custom_call_target="tpu_custom_call" | custom-call | tf_op jit(solution)/shard_map/exchange/pallas_call | solution.py:373
  41.5 1.1 %finish.1 = (f32[4,5,16,8,128]{4,3,2,1,0:T(8,128)}, f32[2,2,2,2]{3,2,1,0:T(2,128)}) custom-call(f32[4,5,16,8,128]{4,3,2,1,0:T(8,128)S(1)} %get-tuple-element.6.spectra, f32[16,1,128]{2,1,0:T(1,128)S(1)} %get-tuple-element.7.gram_in), custom_call_target="tpu_custom_call" | custom-call | tf_op jit(solution)/shard_map/finish/pallas_call | solution.py:418

commit v7 on v5

--- a/solution.py
+++ b/solution.py
@@ -272,6 +272,11 @@
     def _():
         arrive(last)
 
+    def send_early(v, carry):
+        send_back(v)
+        return carry
+
+    lax.fori_loop(0, 2, send_early, 0)
     transform(last)
 
     shape = (RETAINED_MODES, LANES)
@@ -292,11 +297,7 @@
             src_ref=gram_mine, dst_ref=gram_seen.at[place], send_sem=gram_send, recv_sem=gram_recv,
             device_id={"px": p, "py": z}, device_id_type=MESH,
         ).start()
-    def send_early(v, carry):
-        send_back(v)
-        return carry
-
-    lax.fori_loop(0, VARS - 1, send_early, 0)
+    lax.fori_loop(2, VARS - 1, send_early, 0)
     lay_out(VARS - 1)
     send_back(VARS - 1)
 
@@ -308,7 +309,6 @@
                 spectra[i, v, k] = held[v, k, i].astype(jnp.float32) * by
         return carry
 
-    lax.fori_loop(0, 2, scale, 0)
     pltpu.make_async_copy(gram_seen.at[pl.ds(0, n_planes)], gram_seen.at[pl.ds(0, n_planes)], gram_recv).wait()
     whole = jnp.sum(gram_seen[...], axis=0)
     gram_sum[...] = whole
@@ -318,7 +318,7 @@
             src_ref=gram_sum, dst_ref=gram_out.at[me], send_sem=last_send, recv_sem=last_recv,
             device_id={"ta": peer}, device_id_type=MESH,
         ).start()
-    lax.fori_loop(2, VARS, scale, 0)
+    lax.fori_loop(0, VARS, scale, 0)
     pltpu.make_async_copy(gram_out.at[pl.ds(0, n)], gram_out.at[pl.ds(0, n)], last_recv).wait()
     for v in range(last):
         pltpu.make_async_copy(arrived.at[v, pl.ds(0, n)], arrived.at[v, pl.ds(0, n)], send_sem.at[v]).wait()

time: 42.6 us -> 42.9 us (level)
  no operation moved by 1% of the time
where the time goes in v7:
time: 42.9 us; the launch traced here: 42.8 us
  Pallas kernels  42.1 us (98%)
  between operations  0.64 us (1%)
    pallas_call x1, Pallas kernels, on_device(): pl.pallas_call(functools.partial(exchange_kernel, groups, width, cores, d...  41 us
    pallas_call x1, Pallas kernels, on_device(): pl.pallas_call(functools.partial(finish_kernel, total), name='finish', ou...  1.1 us

profile of v7, /device:TPU:1, one launch (start us, length us, event | category | flops | bytes accessed | tf_op | source)
XLA Modules:
  0.0 42.8 jit_solution(3974572288938894742)
XLA Ops:
  0.6 41.0 %exchange.1 = (f32[4,5,16,8,128]{4,3,2,1,0:T(8,128)S(1)}, f32[16,1,128]{2,1,0:T(1,128)S(1)}) custom-call(bf16[5,24,8192]{2,1,0:T(8,128)(2,1)} %bitcast.7, f32[64,128]{1,0:T(8,128)} %bitcast.8, s32[32]{0:T(128)} %indices.1), custom_call_target="tpu_custom_call" | custom-call | tf_op jit(solution)/shard_map/exchange/pallas_call | solution.py:373
  41.7 1.1 %finish.1 = (f32[4,5,16,8,128]{4,3,2,1,0:T(8,128)}, f32[2,2,2,2]{3,2,1,0:T(2,128)}) custom-call(f32[4,5,16,8,128]{4,3,2,1,0:T(8,128)S(1)} %get-tuple-element.6.spectra, f32[16,1,128]{2,1,0:T(1,128)S(1)} %get-tuple-element.7.gram_in), custom_call_target="tpu_custom_call" | custom-call | tf_op jit(solution)/shard_map/finish/pallas_call | solution.py:418

commit v8 on v7

--- a/solution.py
+++ b/solution.py
@@ -220,7 +220,7 @@
         for j in range(tiles):
             w = w_ref[pl.ds(me * tiles + j, 1), :]
             cut = slice(j * LANES, (j + 1) * LANES)
-            r0, r1, i0, i1 = (terms[32 * i : 32 * i + 32, cut] for i in range(4))
+            r0, r1, i0, i1 = (raw[32 * i : 32 * i + 32, cut] for i in range(4))
             total[0] += (r0 * r0 + i0 * i0) * w
             total[1] += (r1 * r1 + i1 * i1) * w
             total[2] += (r0 * r1 + i0 * i1) * w
@@ -276,7 +276,7 @@
         send_back(v)
         return carry
 
-    lax.fori_loop(0, 2, send_early, 0)
+    lax.fori_loop(0, VARS - 1, send_early, 0)
     transform(last)
 
     shape = (RETAINED_MODES, LANES)
@@ -297,7 +297,6 @@
             src_ref=gram_mine, dst_ref=gram_seen.at[place], send_sem=gram_send, recv_sem=gram_recv,
             device_id={"px": p, "py": z}, device_id_type=MESH,
         ).start()
-    lax.fori_loop(2, VARS - 1, send_early, 0)
     lay_out(VARS - 1)
     send_back(VARS - 1)
 

time: 42.9 us -> 43 us (level)
  no operation moved by 1% of the time
where the time goes in v8:
time: 43 us; the launch traced here: 42.9 us
  Pallas kernels  42.2 us (98%)
  between operations  0.64 us (1%)
    pallas_call x1, Pallas kernels, on_device(): pl.pallas_call(functools.partial(exchange_kernel, groups, width, cores, d...  41.1 us
    pallas_call x1, Pallas kernels, on_device(): pl.pallas_call(functools.partial(finish_kernel, total), name='finish', ou...  1.1 us

profile of v8, /device:TPU:1, one launch (start us, length us, event | category | flops | bytes accessed | tf_op | source)
XLA Modules:
  0.0 42.9 jit_solution(2435016405200149844)
XLA Ops:
  0.6 41.1 %exchange.1 = (f32[4,5,16,8,128]{4,3,2,1,0:T(8,128)S(1)}, f32[16,1,128]{2,1,0:T(1,128)S(1)}) custom-call(bf16[5,24,8192]{2,1,0:T(8,128)(2,1)} %bitcast.7, f32[64,128]{1,0:T(8,128)} %bitcast.8, s32[32]{0:T(128)} %indices.1), custom_call_target="tpu_custom_call" | custom-call | tf_op jit(solution)/shard_map/exchange/pallas_call | solution.py:372
  41.8 1.1 %finish.1 = (f32[4,5,16,8,128]{4,3,2,1,0:T(8,128)}, f32[2,2,2,2]{3,2,1,0:T(2,128)}) custom-call(f32[4,5,16,8,128]{4,3,2,1,0:T(8,128)S(1)} %get-tuple-element.6.spectra, f32[16,1,128]{2,1,0:T(1,128)S(1)} %get-tuple-element.7.gram_in), custom_call_target="tpu_custom_call" | custom-call | tf_op jit(solution)/shard_map/finish/pallas_call | solution.py:417
